TPU v7x, 256 devices: a whole 4x4x8 slice. The times are simulated.
256 devices in a mesh: seq: 64 (over x_hi, y, z), tp: 4 (over x_lo, core).
Axes of the slice: x: 4 (x_hi: 2, x_lo: 2; x = x_hi * 2 + x_lo), y: 4, z: 8, core: 2. Of those that a mesh axis runs over, the one named last changes fastest.
Arguments:
- mixer_input: bfloat16 [8192, 8192], P('seq', 'tp'), may hold values from -6 to 6
- gate_input: bfloat16 [8192, 8192], P('seq', 'tp'), may hold values from -6 to 6
- input_matrix: bfloat16 [8192, 1024], P('seq', 'tp'), may hold values from -6 to 6
- output_matrix: bfloat16 [8192, 1024], P('seq', 'tp'), may hold values from -6 to 6
- step_raw: float32 [8192, 128], P('seq', 'tp'), may hold values from -3 to 3
- step_bias: float32 [128], P('tp'), may hold values from -1 to 0.5
- decay_rate: float32 [128], P('tp'), may hold values from 0.0001 to 0.05
- skip_weight: float32 [128], P('tp'), may hold values from 0.5 to 1.5
- conv_mixer: float32 [4, 8192], P(None, 'tp'), may hold values from -3 to 3
- conv_input: float32 [4, 1024], P(None, 'tp'), may hold values from -3 to 3
- conv_output: float32 [4, 1024], P(None, 'tp'), may hold values from -3 to 3
- norm_gain: float32 [8192], P('tp'), may hold values from 0.5 to 1.5
- queries: bfloat16 [8192, 8192], P('seq', 'tp'), may hold values from -5 to 5
- keys: bfloat16 [8192, 1024], P('seq', 'tp'), may hold values from -5 to 5
- values: bfloat16 [8192, 1024], P('seq', 'tp'), may hold values from -6 to 6
Outputs:
- mixer_out: bfloat16 [8192, 8192], P('seq', 'tp')
- attention_out: bfloat16 [8192, 8192], P('seq', 'tp')
All inputs are finite; a program needn't handle non-finite values.
Results may differ from a plain program's by a relative error of at most 0.007.
Values may be sent and summed in bfloat16 or wider, within the bound.
A program may use at most 192 MiB of HBM per device.

v0:
```python
import math

import jax
import jax.numpy as jnp
from jax import lax
from jax.sharding import Mesh
from jax.sharding import PartitionSpec as P

MH = 128
P_SIZE = 64
STATE = 128
HD = 128
CONV = 4
SEQ = ("seq_0", "seq_1", "seq_2")


norm_epsilon = 1e-05
lowest_score = -1e30


def from_behind(value, axis, by):
    size = lax.axis_size(axis)
    pairs = [(i, i + by) for i in range(size) if 0 <= i + by < size]
    return lax.ppermute(value, axis, pairs)


def neutral_like(value, identity):
    return jax.tree.map(
        lambda part, zero: jnp.zeros_like(part) + jnp.asarray(zero, part.dtype), value, identity
    )


def entering_2(value, axes, combine, identity):
    before = start = neutral_like(value, identity)
    subtotal = value
    for axis in reversed(axes):
        size, mine = (lax.axis_size(axis), lax.axis_index(axis))
        pieces = jax.tree.map(lambda part: lax.all_gather(part, axis), subtotal)
        inside, subtotal = (start, start)
        for k in range(size):
            passed = k < mine
            subtotal = combine(subtotal, jax.tree.map(lambda part: part[k], pieces))
            inside = jax.tree.map(lambda new, old: jnp.where(passed, new, old), subtotal, inside)
        before = combine(inside, before)
    return before


def from_everyone(value, axis):
    size = lax.axis_size(axis)
    return lax.all_to_all(
        jnp.broadcast_to(value[None], (size, *value.shape)), axis, 0, 0, tiled=True
    )


def taken_together(value, axis):
    return from_everyone(value, axis).sum(axis=0)


def partner(block, axis, distance):
    count = lax.axis_size(axis)
    route = []
    for low in range(count):
        high = low | 1 << distance
        if high != low and high < count:
            route += [(low, high), (high, low)]
    return lax.ppermute(block, axis, route)


def in_one_piece(arrays, axis, dim, along):
    both = jnp.concatenate(arrays, axis=along)
    result, at, gathered = (lax.all_gather(both, axis, axis=dim, tiled=True), 0, [])
    for a in arrays:
        gathered.append(lax.slice_in_dim(result, at, at + a.shape[along], axis=along))
        at += a.shape[along]
    return tuple(gathered)


def conv_silu(raw_rows, weights, history):
    padded = jnp.concatenate([history, raw_rows], axis=0).astype(jnp.float32)
    length = raw_rows.shape[0]
    summed = jnp.zeros((length, raw_rows.shape[1]), jnp.float32)
    for offset in range(weights.shape[0]):
        summed = summed + weights[offset][None, :] * padded[offset : offset + length]
    return jax.nn.silu(summed)


def ssd_block(signal, b_state, c_state, step_size, rates, carried):
    group_heads = signal.shape[1] // b_state.shape[1]
    log_decay = jnp.cumsum(-step_size * rates[None, :], axis=0)
    length = signal.shape[0]
    places = jnp.arange(length, dtype=jnp.int32)
    causal = (places[:, None] >= places[None, :])[:, :, None]
    spread = jnp.where(causal, log_decay[:, None, :] - log_decay[None, :, :], 0.0)
    decays = jnp.where(causal, jnp.exp(spread), 0.0)
    coupling = jnp.einsum("tgn,sgn->gts", c_state, b_state)
    coupling = jnp.repeat(coupling, group_heads, axis=0)
    mixing = jnp.transpose(decays, (2, 0, 1)) * coupling
    scaled = signal * step_size[:, :, None]
    output = jnp.einsum("hts,shp->thp", mixing, scaled)
    b_heads = jnp.repeat(b_state, group_heads, axis=1)
    c_heads = jnp.repeat(c_state, group_heads, axis=1)
    output = output + jnp.exp(log_decay)[:, :, None] * jnp.einsum("thn,hpn->thp", c_heads, carried)
    closing = jnp.exp(log_decay[-1][None, :] - log_decay)
    weighted = scaled * closing[:, :, None]
    updated = jnp.exp(log_decay[-1])[:, None, None] * carried + jnp.einsum(
        "shp,shn->hpn", weighted, b_heads
    )
    return (output, updated, log_decay, c_heads)


def combine_states(earlier, later):
    return (earlier[0] * later[0], later[0][:, None, None] * earlier[1] + later[1])


def attend_update(carry, query_block, query_start, key_block, value_block, key_start):
    maxima, totals, accum = carry
    kv_heads = key_block.shape[1] // HD
    grouped = query_block.shape[1] // HD // kv_heads
    query_rows = query_block.shape[0]
    key_rows = key_block.shape[0]
    query_four = query_block.reshape(query_rows, kv_heads, grouped, HD)
    key_three = key_block.reshape(key_rows, kv_heads, HD)
    value_three = value_block.reshape(key_rows, kv_heads, HD)
    scores = jnp.einsum("qhgd,khd->hgqk", query_four, key_three, preferred_element_type=jnp.float32)
    scores = scores * (1.0 / math.sqrt(HD))
    query_places = query_start + jnp.arange(query_rows, dtype=jnp.int32)
    key_places = key_start + jnp.arange(key_rows, dtype=jnp.int32)
    allowed = key_places[None, :] <= query_places[:, None]
    masked = jnp.where(allowed, scores, lowest_score)
    newmax = jnp.maximum(maxima, jnp.max(masked, axis=-1))
    probs = jnp.where(allowed, jnp.exp(masked - newmax[..., None]), 0.0)
    factor = jnp.exp(maxima - newmax)
    totals = totals * factor + jnp.sum(probs, axis=-1)
    rounded = probs.astype(jnp.bfloat16)
    product = jnp.einsum("hgqk,khd->hgqd", rounded, value_three, preferred_element_type=jnp.float32)
    accum = accum * factor[..., None] + product
    return (newmax, totals, accum)


def finish(carry):
    maxima, totals, accum = carry
    result = accum / totals[..., None]
    result = jnp.transpose(result, (2, 0, 1, 3))
    return result.reshape(result.shape[0], -1).astype(jnp.bfloat16)


def mixer_local(
    mixer_input,
    gate_input,
    input_matrix,
    output_matrix,
    step_raw,
    step_bias,
    decay_rate,
    skip_weight,
    conv_mixer,
    conv_input,
    conv_output,
    norm_gain,
):
    reach = CONV - 1
    history = from_behind(
        (mixer_input[-reach:], input_matrix[-reach:], output_matrix[-reach:]), SEQ, 1
    )
    length = mixer_input.shape[0]
    heads = mixer_input.shape[1] // P_SIZE
    groups = input_matrix.shape[1] // STATE
    signal = conv_silu(mixer_input, conv_mixer, history[0]).reshape(length, heads, P_SIZE)
    b_state = conv_silu(input_matrix, conv_input, history[1]).reshape(length, groups, STATE)
    c_state = conv_silu(output_matrix, conv_output, history[2]).reshape(length, groups, STATE)
    step_size = jax.nn.softplus(step_raw + step_bias[None, :])
    carried = jnp.zeros((heads, P_SIZE, STATE), jnp.float32)
    output, carried, log_decay, c_heads = ssd_block(
        signal, b_state, c_state, step_size, decay_rate, carried
    )
    offset_log = log_decay[-1]
    device_decay = jnp.exp(offset_log)
    identity = (jnp.ones((heads,), jnp.float32), jnp.zeros((heads, P_SIZE, STATE), jnp.float32))
    prefix_decay, entering = entering_2((device_decay, carried), SEQ, combine_states, identity)
    mixed = output
    mixed = mixed + jnp.exp(log_decay)[:, :, None] * jnp.einsum("thn,hpn->thp", c_heads, entering)
    mixed = mixed + skip_weight[None, :, None] * signal
    gated = mixed.reshape(length, heads * P_SIZE) * jax.nn.silu(gate_input.astype(jnp.float32))
    squares = taken_together(jnp.sum(gated * gated, axis=1), "tp")
    scaling = lax.rsqrt(squares / (MH * P_SIZE) + norm_epsilon)
    return (gated * scaling[:, None] * norm_gain[None, :]).astype(jnp.bfloat16)


def attend_local(queries, keys, values):
    length = queries.shape[0]
    half_len = length // 2
    device = lax.axis_index(SEQ)
    count = lax.axis_size(SEQ)
    own_start = device * length
    near_rows = queries[:half_len]
    far_rows = queries[half_len:]
    for bit_index in range(count.bit_length() - 1):
        far_rows = partner(far_rows, SEQ, bit_index)
    far_start = (count - 1 - device) * length + half_len
    kv_heads = keys.shape[1] // HD
    grouped = queries.shape[1] // HD // kv_heads

    def fresh():
        return (
            jnp.full((kv_heads, grouped, half_len), lowest_score, jnp.float32),
            jnp.zeros((kv_heads, grouped, half_len), jnp.float32),
            jnp.zeros((kv_heads, grouped, half_len, HD), jnp.float32),
        )

    key_piece, value_piece = in_one_piece((keys, values), SEQ, 0, 1)
    span = math.gcd(key_piece.shape[0], 512)

    def visit(position, inner):
        key_start = position * span
        key_block = lax.dynamic_slice_in_dim(key_piece, position * span, span, 0)
        value_block = lax.dynamic_slice_in_dim(value_piece, position * span, span, 0)
        near_state = lax.cond(
            key_start <= own_start + half_len - 1,
            lambda carry_in: attend_update(
                carry_in, near_rows, own_start, key_block, value_block, key_start
            ),
            lambda carry_in: carry_in,
            inner[0],
        )
        far_state = lax.cond(
            key_start <= far_start + half_len - 1,
            lambda carry_in: attend_update(
                carry_in, far_rows, far_start, key_block, value_block, key_start
            ),
            lambda carry_in: carry_in,
            inner[1],
        )
        return (near_state, far_state)

    near_state, far_state = lax.fori_loop(0, key_piece.shape[0] // span, visit, (fresh(), fresh()))
    near_out = finish(near_state)
    far_out = finish(far_state)
    for bit_index in range(count.bit_length() - 1):
        far_out = partner(far_out, SEQ, bit_index)
    return jnp.concatenate([near_out, far_out], axis=0)


def shards(
    mixer_input,
    gate_input,
    input_matrix,
    output_matrix,
    step_raw,
    step_bias,
    decay_rate,
    skip_weight,
    conv_mixer,
    conv_input,
    conv_output,
    norm_gain,
    queries,
    keys,
    values,
):
    mixer_out = mixer_local(
        mixer_input,
        gate_input,
        input_matrix,
        output_matrix,
        step_raw,
        step_bias,
        decay_rate,
        skip_weight,
        conv_mixer,
        conv_input,
        conv_output,
        norm_gain,
    )
    attention_out = attend_local(queries, keys, values)
    return (mixer_out, attention_out)


def solution(mesh):
    torus = Mesh(mesh.devices.reshape(2, 4, 8, mesh.shape["tp"]), ("seq_0", "seq_1", "seq_2", "tp"))
    placed = (
        P(SEQ, "tp"),
        P(SEQ, "tp"),
        P(SEQ, "tp"),
        P(SEQ, "tp"),
        P(SEQ, "tp"),
        P("tp"),
        P("tp"),
        P("tp"),
        P(None, "tp"),
        P(None, "tp"),
        P(None, "tp"),
        P("tp"),
        P(SEQ, "tp"),
        P(SEQ, "tp"),
        P(SEQ, "tp"),
    )
    return jax.shard_map(
        shards, mesh=torus, in_specs=placed, out_specs=(P(SEQ, "tp"), P(SEQ, "tp")), check_vma=False
    )
```

profile of v0, /device:TPU:1, one launch (start us, length us, event | category | flops | bytes accessed | tf_op | source)
XLA Modules:
  0.0 486.6 jit_solution(17566430420498591905)
XLA Ops:
  7.9 4.3 collective-permute-start.2
  26.5 12.4 %all-gather.1 = f32[8,1,32]{2,1,0:T(1,128)S(1)} all-gather(f32[1,1,32]{2,1,0:T(1,128)S(1)} %get-tuple-element.504), channel_id=1, replica_groups=mesh['seq_0'=2,'seq_1'=4,'seq_2'=8,'tp'=4] {'seq_2'}, dimensions={0}, use_global_device_ids=true | all-gather | bytes 1152 | tf_op jit(solution)/shard_map/all_gather | solution.py:38
  39.0 82.5 %all-gather.15.cloned.1.call-done = f32[256,64,128]{2,1,0:T(8,128)} async-done(((f32[32,64,128]{2,1,0:T(8,128)}), f32[256,64,128]{2,1,0:T(8,128)}) %all-gather.15.cloned.1.call-update) | async-done | bytes 8388624 | tf_op jit(solution)/shard_map/all_gather | solution.py:38
  121.5 4.6 bitcast_add_fusion.4
  126.4 7.0 %collective-permute-done.3 = bf16[64,2048]{1,0:T(8,128)(2,1)S(1)} collective-permute-done((bf16[64,2048]{1,0:T(8,128)(2,1)S(1)}, bf16[64,2048]{1,0:T(8,128)(2,1)S(1)}, u32[]{:S(2)}, u32[]{:S(2)}) %collective-permute-start.3) | collective-permute-done | bytes 262176 | tf_op jit(solution)/shard_map/ppermute | solution.py:66
  135.2 13.7 %collective-permute-done.4 = bf16[64,2048]{1,0:T(8,128)(2,1)S(1)} collective-permute-done((bf16[64,2048]{1,0:T(8,128)(2,1)S(1)}, bf16[64,2048]{1,0:T(8,128)(2,1)S(1)}, u32[]{:S(2)}, u32[]{:S(2)}) %collective-permute-start.4) | collective-permute-done | bytes 262176 | tf_op jit(solution)/shard_map/ppermute | solution.py:66
  150.9 16.0 %collective-permute-done.5 = bf16[64,2048]{1,0:T(8,128)(2,1)S(1)} collective-permute-done((bf16[64,2048]{1,0:T(8,128)(2,1)S(1)}, bf16[64,2048]{1,0:T(8,128)(2,1)S(1)}, u32[]{:S(2)}, u32[]{:S(2)}) %collective-permute-start.5) | collective-permute-done | bytes 262176 | tf_op jit(solution)/shard_map/ppermute | solution.py:66
  168.0 9.6 %all-gather.2 = f32[4,1,32]{2,1,0:T(1,128)S(1)} all-gather(f32[1,1,32]{2,1,0:T(1,128)S(1)} %fusion.151), channel_id=1, replica_groups=mesh['seq_0'=2,'seq_1'=4,'seq_2'=8,'tp'=4] {'seq_1'}, dimensions={0}, use_global_device_ids=true | all-gather | bytes 640 | tf_op jit(solution)/shard_map/all_gather | solution.py:38
  179.2 5.4 %collective-permute-done.7 = bf16[64,2048]{1,0:T(8,128)(2,1)S(1)} collective-permute-done((bf16[64,2048]{1,0:T(8,128)(2,1)S(1)}, bf16[64,2048]{1,0:T(8,128)(2,1)S(1)}, u32[]{:S(2)}, u32[]{:S(2)}) %collective-permute-start.7) | collective-permute-done | bytes 262176 | tf_op jit(solution)/shard_map/ppermute | solution.py:66
  184.6 4.5 collective-permute-start.8
  189.1 93.2 %all-gather.13.cloned.1.call-done = bf16[8192,512]{1,0:T(8,128)(2,1)} async-done(((bf16[128,512]{1,0:T(8,128)(2,1)}), bf16[8192,512]{1,0:T(8,128)(2,1)}) %all-gather.13.cloned.1.call-update) | async-done | bytes 8388624 | tf_op jit(solution)/shard_map/all_gather | solution.py:71
  282.3 5.8 %fusion.155 = (bf16[8192,256]{1,0:T(8,128)(2,1)}, bf16[8192,256]{1,0:T(8,128)(2,1)}) fusion(bf16[8192,512]{1,0:T(8,128)(2,1)} %all-gather.13.cloned.1.call-done), kind=kLoop, calls=%fused_computation.259 | loop fusion | bytes 16777216 | tf_op jit(solution)/shard_map/slice | solution.py:73
  289.9 90.3 %while.26 = (s32[]{:T(128)}, f32[2,8,64]{2,1,0:T(8,128)S(1)}, f32[2,8,64]{2,1,0:T(8,128)S(1)}, f32[2,8,64,128]{3,2,1,0:T(8,128)}, f32[2,8,64]{2,1,0:T(8,128)S(1)...) while((s32[]{:T(128)}, f32[2,8,64]{2,1,0:T(8,128)S(1)}, ...), condition=%wide.region_12.13_spmd, body=%wide.region_3.12_spmd.sunk | while | flops 551097472 | bytes 20850180 | solution.py:235
  291.0 5.8 %conditional.4 = ((f32[2,8,64]{2,1,0:T(8,128)S(1)}, f32[2,8,64]{2,1,0:T(8,128)S(1)}, f32[2,8,64,128]{3,2,1,0:T(8,128)})) conditional(s32[]{:T(128)} %convert_element_type.102, (f32[2,8,64]{2,1,0:T(8,128)S(1)}, f32[2,8,64]{2,1,0:T(8,128)S(1)}, f32[2,8,64,128]{3,2,1,0:T(8,128)}) %tuple.93, (s32[]{:T(128)}, s32[]{:T(128)}, ...), branch_computations={%region_4.4_spmd, %region_5.7_spmd} | conditional | flops 275548736 | bytes 9900584 | solution.py:217
  296.8 4.2 conditional.5
  312.7 4.2 conditional.5
  323.2 4.2 conditional.5
  393.4 15.1 %all-gather.3 = f32[2,1,32]{2,1,0:T(1,128)S(1)} all-gather(f32[1,1,32]{2,1,0:T(1,128)S(1)} %copy-done.47), channel_id=1, replica_groups=mesh['seq_0'=2,'seq_1'=4,'seq_2'=8,'tp'=4] {'seq_0'}, dimensions={0}, use_global_device_ids=true | all-gather | bytes 384 | tf_op jit(solution)/shard_map/all_gather | solution.py:38
  412.4 5.4 %collective-permute-done.11 = bf16[64,2048]{1,0:T(8,128)(2,1)S(1)} collective-permute-done((bf16[64,2048]{1,0:T(8,128)(2,1)S(1)}, bf16[64,2048]{1,0:T(8,128)(2,1)S(1)}, u32[]{:S(2)}, u32[]{:S(2)}) %collective-permute-start.11) | collective-permute-done | bytes 262176 | tf_op jit(solution)/shard_map/ppermute | solution.py:66
  417.8 4.4 collective-permute-start.12
  426.4 8.8 %collective-permute-start.13 = (bf16[64,2048]{1,0:T(8,128)(2,1)S(1)}, bf16[64,2048]{1,0:T(8,128)(2,1)}, u32[]{:S(2)}, u32[]{:S(2)}) collective-permute-start(bf16[64,2048]{1,0:T(8,128)(2,1)S(1)} %collective-permute-done.12), channel_id=1, source_target_pairs={{0,64},{64,0},{4,68},{68,4},{8,72},{72,8},{12,76},{76,12},{16,80},... | collective-permute-start | bytes 786440 | tf_op jit(solution)/shard_map/ppermute | solution.py:66
  439.3 13.5 %collective-permute-start.14 = (bf16[64,2048]{1,0:T(8,128)(2,1)}, bf16[64,2048]{1,0:T(8,128)(2,1)}, u32[]{:S(2)}, u32[]{:S(2)}) collective-permute-start(bf16[64,2048]{1,0:T(8,128)(2,1)} %collective-permute-done.13), channel_id=1, source_target_pairs={{0,128},{128,0},{4,132},{132,4},{8,136},{136,8},{12,140},{140,12},... | collective-permute-start | bytes 786440 | tf_op jit(solution)/shard_map/ppermute | solution.py:66
  453.0 6.5 %fusion.30 = f32[128,32,64]{0,2,1:T(8,128)S(1)} fusion(bf16[128,32,128]{2,0,1:T(8,128)(2,1)S(1)} %bitcast.291, f32[2,32,64,128]{3,2,1,0:T(8,128)} %all-gather.11.cloned.1.call-done, f32[4,32,64,128]{3,2,1,0:T(8,128)} %all-gather.9.cloned.1.call-done, f32[256,64,128]{2,1,0:T(8,128)} %all-gather.15.cloned.1.call-done, f32[32]{0:T(128)S(1)} %copy-done.45, ...), kind=kOutput, calls=%fused_computation.48 | convolution fusion | flops 78643200 | bytes 16795662 | tf_op jit(solution)/shard_map/thn,hpn->thp/dot_general | solution.py:181
  464.1 11.7 %all-to-all-start = ((f32[4,1,128]{2,1,0:T(1,128)}), f32[4,1,128]{2,1,0:T(1,128)S(1)}, u32[]{:S(2)}, u32[]{:S(2)}) async-start(f32[4,1,128]{2,1,0:T(1,128)} %broadcast_in_dim.91), calls=%async_computation | async-start | bytes 4096 | tf_op jit(solution)/shard_map/all_to_all | solution.py:50
  (435 shorter events, 200.3 us)
Async XLA Ops:
  7.2 114.3 %all-gather.15.cloned.1.call-start = ((), (), s32[]{:S(2)}) async-start(), calls=%async_computation.4 | async-start | bytes 9437184 | tf_op jit(solution)/shard_map/all_gather | solution.py:38
  7.9 12.3 %collective-permute-start.2 = (bf16[3,256]{1,0:T(4,128)(2,1)S(1)}, bf16[3,256]{1,0:T(4,128)(2,1)S(1)}, u32[]{:S(2)}, u32[]{:S(2)}) collective-permute-start(bf16[3,256]{1,0:T(4,128)(2,1)S(1)} %slice.201), channel_id=1, source_target_pairs={{0,4},{4,8},{8,12},{12,16},{16,20},{20,24},{24,28},{28,32},{32,36}... | collective-permute-start | bytes 4616 | tf_op jit(solution)/shard_map/ppermute | solution.py:24
  13.0 8.7 %collective-permute-start = (bf16[3,2048]{1,0:T(4,128)(2,1)S(1)}, bf16[3,2048]{1,0:T(4,128)(2,1)S(1)}, u32[]{:S(2)}, u32[]{:S(2)}) collective-permute-start(bf16[3,2048]{1,0:T(4,128)(2,1)S(1)} %slice.183), channel_id=1, source_target_pairs={{0,4},{4,8},{8,12},{12,16},{16,20},{20,24},{24,28},{28,32},{32,36}... | collective-permute-start | bytes 36872 | tf_op jit(solution)/shard_map/ppermute | solution.py:24
  25.7 256.6 %all-gather.13.cloned.1.call-start = ((), (), s32[]{:S(2)}) async-start(), calls=%async_computation.3 | async-start | bytes 8519680 | tf_op jit(solution)/shard_map/all_gather | solution.py:71
  26.4 353.8 %all-gather.9.cloned.1.call-start = ((), (), s32[]{:S(2)}) async-start(), calls=%async_computation.1 | async-start | bytes 5242880 | tf_op jit(solution)/shard_map/all_gather | solution.py:38
  38.9 129.1 %copy-start.13 = (f32[8,1,32]{2,1,0:T(1,128)}, f32[8,1,32]{2,1,0:T(1,128)S(1)}, u32[]{:S(2)}) copy-start(f32[8,1,32]{2,1,0:T(1,128)S(1)} %all-gather.1) | copy-start | bytes 3076
  38.9 87.2 %copy-start.44 = (f32[32]{0:T(128)}, f32[32]{0:T(128)S(1)}, u32[]{:S(2)}) copy-start(f32[32]{0:T(128)S(1)} %bitcast_multiply_fusion.1) | copy-start | bytes 388
  38.9 87.2 %copy-start.27 = (f32[32]{0:T(128)}, f32[32]{0:T(128)S(1)}, u32[]{:S(2)}) copy-start(f32[32]{0:T(128)S(1)} %get-tuple-element.510) | copy-start | bytes 388
  126.2 326.7 %all-gather.11.cloned.1.call-start = ((), (), s32[]{:S(2)}) async-start(), calls=%async_computation.2 | async-start | bytes 3145728 | tf_op jit(solution)/shard_map/all_gather | solution.py:38
  126.3 7.1 %collective-permute-start.3 = (bf16[64,2048]{1,0:T(8,128)(2,1)S(1)}, bf16[64,2048]{1,0:T(8,128)(2,1)S(1)}, u32[]{:S(2)}, u32[]{:S(2)}) collective-permute-start(bf16[64,2048]{1,0:T(8,128)(2,1)S(1)} %get-tuple-element.500), channel_id=1, source_target_pairs={{0,4},{4,0},{8,12},{12,8},{16,20},{20,16},{24,28},{28,24},{32,36},... | collective-permute-start | bytes 786440 | tf_op jit(solution)/shard_map/ppermute | solution.py:66
  133.4 15.5 %collective-permute-start.4 = (bf16[64,2048]{1,0:T(8,128)(2,1)S(1)}, bf16[64,2048]{1,0:T(8,128)(2,1)S(1)}, u32[]{:S(2)}, u32[]{:S(2)}) collective-permute-start(bf16[64,2048]{1,0:T(8,128)(2,1)S(1)} %collective-permute-done.3), channel_id=1, source_target_pairs={{0,8},{8,0},{4,12},{12,4},{16,24},{24,16},{20,28},{28,20},{32,40},... | collective-permute-start | bytes 786440 | tf_op jit(solution)/shard_map/ppermute | solution.py:66
  148.9 18.0 %collective-permute-start.5 = (bf16[64,2048]{1,0:T(8,128)(2,1)S(1)}, bf16[64,2048]{1,0:T(8,128)(2,1)S(1)}, u32[]{:S(2)}, u32[]{:S(2)}) collective-permute-start(bf16[64,2048]{1,0:T(8,128)(2,1)S(1)} %collective-permute-done.4), channel_id=1, source_target_pairs={{0,16},{16,0},{4,20},{20,4},{8,24},{24,8},{12,28},{28,12},{32,48},... | collective-permute-start | bytes 786440 | tf_op jit(solution)/shard_map/ppermute | solution.py:66
  166.9 10.7 %collective-permute-start.6 = (bf16[64,2048]{1,0:T(8,128)(2,1)S(1)}, bf16[64,2048]{1,0:T(8,128)(2,1)S(1)}, u32[]{:S(2)}, u32[]{:S(2)}) collective-permute-start(bf16[64,2048]{1,0:T(8,128)(2,1)S(1)} %collective-permute-done.5), channel_id=1, source_target_pairs={{0,32},{32,0},{4,36},{36,4},{8,40},{40,8},{12,44},{44,12},{16,48},... | collective-permute-start | bytes 786440 | tf_op jit(solution)/shard_map/ppermute | solution.py:66
  177.5 110.6 %copy-start.15 = (f32[4,1,32]{2,1,0:T(1,128)}, f32[4,1,32]{2,1,0:T(1,128)S(1)}, u32[]{:S(2)}) copy-start(f32[4,1,32]{2,1,0:T(1,128)S(1)} %all-gather.2) | copy-start | bytes 1540
  177.5 7.0 %collective-permute-start.7 = (bf16[64,2048]{1,0:T(8,128)(2,1)S(1)}, bf16[64,2048]{1,0:T(8,128)(2,1)S(1)}, u32[]{:S(2)}, u32[]{:S(2)}) collective-permute-start(bf16[64,2048]{1,0:T(8,128)(2,1)S(1)} %collective-permute-done.6), channel_id=1, source_target_pairs={{0,64},{64,0},{4,68},{68,4},{8,72},{72,8},{12,76},{76,12},{16,80},... | collective-permute-start | bytes 786440 | tf_op jit(solution)/shard_map/ppermute | solution.py:66
  184.6 103.6 %collective-permute-start.8 = (bf16[64,2048]{1,0:T(8,128)(2,1)S(1)}, bf16[64,2048]{1,0:T(8,128)(2,1)S(1)}, u32[]{:S(2)}, u32[]{:S(2)}) collective-permute-start(bf16[64,2048]{1,0:T(8,128)(2,1)S(1)} %collective-permute-done.7), channel_id=1, source_target_pairs={{0,128},{128,0},{4,132},{132,4},{8,136},{136,8},{12,140},{140,12},... | collective-permute-start | bytes 786440 | tf_op jit(solution)/shard_map/ppermute | solution.py:66
  385.6 5.3 %collective-permute-start.9 = (bf16[64,2048]{1,0:T(8,128)(2,1)S(1)}, bf16[64,2048]{1,0:T(8,128)(2,1)S(1)}, u32[]{:S(2)}, u32[]{:S(2)}) collective-permute-start(bf16[64,2048]{1,0:T(8,128)(2,1)S(1)} %bitcast.298), channel_id=1, source_target_pairs={{0,4},{4,0},{8,12},{12,8},{16,20},{20,16},{24,28},{28,24},{32,36},... | collective-permute-start | bytes 786440 | tf_op jit(solution)/shard_map/ppermute | solution.py:66
  386.8 25.6 %collective-permute-start.1 = (bf16[3,256]{1,0:T(4,128)(2,1)S(1)}, bf16[3,256]{1,0:T(4,128)(2,1)S(1)}, u32[]{:S(2)}, u32[]{:S(2)}) collective-permute-start(bf16[3,256]{1,0:T(4,128)(2,1)S(1)} %slice.192), channel_id=1, source_target_pairs={{0,4},{4,8},{8,12},{12,16},{16,20},{20,24},{24,28},{28,32},{32,36}... | collective-permute-start | bytes 4616 | tf_op jit(solution)/shard_map/ppermute | solution.py:24
  390.9 17.6 %collective-permute-start.10 = (bf16[64,2048]{1,0:T(8,128)(2,1)S(1)}, bf16[64,2048]{1,0:T(8,128)(2,1)S(1)}, u32[]{:S(2)}, u32[]{:S(2)}) collective-permute-start(bf16[64,2048]{1,0:T(8,128)(2,1)S(1)} %collective-permute-done.9), channel_id=1, source_target_pairs={{0,8},{8,0},{4,12},{12,4},{16,24},{24,16},{20,28},{28,20},{32,40},... | collective-permute-start | bytes 786440 | tf_op jit(solution)/shard_map/ppermute | solution.py:66
  408.5 9.3 %collective-permute-start.11 = (bf16[64,2048]{1,0:T(8,128)(2,1)S(1)}, bf16[64,2048]{1,0:T(8,128)(2,1)S(1)}, u32[]{:S(2)}, u32[]{:S(2)}) collective-permute-start(bf16[64,2048]{1,0:T(8,128)(2,1)S(1)} %collective-permute-done.10), channel_id=1, source_target_pairs={{0,16},{16,0},{4,20},{20,4},{8,24},{24,8},{12,28},{28,12},{32,48},... | collective-permute-start | bytes 786440 | tf_op jit(solution)/shard_map/ppermute | solution.py:66
  417.8 8.6 %collective-permute-start.12 = (bf16[64,2048]{1,0:T(8,128)(2,1)S(1)}, bf16[64,2048]{1,0:T(8,128)(2,1)S(1)}, u32[]{:S(2)}, u32[]{:S(2)}) collective-permute-start(bf16[64,2048]{1,0:T(8,128)(2,1)S(1)} %collective-permute-done.11), channel_id=1, source_target_pairs={{0,32},{32,0},{4,36},{36,4},{8,40},{40,8},{12,44},{44,12},{16,48},... | collective-permute-start | bytes 786440 | tf_op jit(solution)/shard_map/ppermute | solution.py:66
  426.4 13.0 %collective-permute-start.13 = (bf16[64,2048]{1,0:T(8,128)(2,1)S(1)}, bf16[64,2048]{1,0:T(8,128)(2,1)}, u32[]{:S(2)}, u32[]{:S(2)}) collective-permute-start(bf16[64,2048]{1,0:T(8,128)(2,1)S(1)} %collective-permute-done.12), channel_id=1, source_target_pairs={{0,64},{64,0},{4,68},{68,4},{8,72},{72,8},{12,76},{76,12},{16,80},... | collective-permute-start | bytes 786440 | tf_op jit(solution)/shard_map/ppermute | solution.py:66
  439.3 36.5 %collective-permute-start.14 = (bf16[64,2048]{1,0:T(8,128)(2,1)}, bf16[64,2048]{1,0:T(8,128)(2,1)}, u32[]{:S(2)}, u32[]{:S(2)}) collective-permute-start(bf16[64,2048]{1,0:T(8,128)(2,1)} %collective-permute-done.13), channel_id=1, source_target_pairs={{0,128},{128,0},{4,132},{132,4},{8,136},{136,8},{12,140},{140,12},... | collective-permute-start | bytes 786440 | tf_op jit(solution)/shard_map/ppermute | solution.py:66
  464.1 14.7 %all-to-all-start = ((f32[4,1,128]{2,1,0:T(1,128)}), f32[4,1,128]{2,1,0:T(1,128)S(1)}, u32[]{:S(2)}, u32[]{:S(2)}) async-start(f32[4,1,128]{2,1,0:T(1,128)} %broadcast_in_dim.91), calls=%async_computation | async-start | bytes 4096 | tf_op jit(solution)/shard_map/all_to_all | solution.py:50
  (45 other events, 1236.2 us)
Sparse Core Ops, SparseCore 0:
  25.8 95.6 all-gather.14
  125.8 156.4 all-gather.12
  284.1 50.4 all-gather.8
  384.0 63.4 all-gather.10
where the time goes:
time: 489 us; the launch traced here: 487 us
  waiting for transfers between devices  232 us (47%)
  starting transfers between devices  66.1 us (14%)
  matrix products  65.1 us (13%)
  blocking collectives  37 us (8%)
  local copies, waits for them, and re-layouts  36 us (7%)
  other arithmetic  33.9 us (7%)
  between operations  14.6 us (3%)
    all_gather x1, waiting for transfers between devices, in_one_piece(): lax.all_gather(both, axis, axis=dim, tiled=True)  93.2 us
    all_gather x3, waiting for transfers between devices, entering_2(): pieces = jax.tree.map(lambda part: lax.all_gather(part, axis), subtotal)  82.5 us
    ppermute x12, waiting for transfers between devices, partner(): return lax.ppermute(block, axis, route)  55 us
    ppermute x12, starting transfers between devices, partner(): return lax.ppermute(block, axis, route)  44 us
    dot_general x17, matrix products, attend_update(): jnp.einsum('hgqk,khd->hgqd', rounded, value_three, preferred_element_type...  43.9 us
    all_gather x3, blocking collectives, entering_2(): pieces = jax.tree.map(lambda part: lax.all_gather(part, axis), subtotal)  37 us
    dynamic_slice x16, local copies, waits for them, and re-layouts, visit(): lax.dynamic_slice_in_dim(value_piece, position * span, span, 0)  17 us
    reduce_sum x17, other arithmetic, attend_update(): totals = totals * factor + jnp.sum(probs, axis=-1)  11.7 us
  transfers between devices with their start and end apart: 20, of which 11 were waited for; matrix products, arithmetic and copies ran while one was open for 26% of the time, Pallas kernels for 0%

commit v1 on v0

v1 whole, which is shorter than its diff:
```python
import functools
import math

import jax
import jax.numpy as jnp
from jax import lax
from jax.experimental import pallas as pl
from jax.experimental.pallas import tpu as pltpu
from jax.sharding import Mesh
from jax.sharding import PartitionSpec as P

P_SIZE = 64
STATE = 128
HD = 128
CONV = 4
SEQ = ("seq_0", "seq_1", "seq_2")
MESH = pl.DeviceIdType.MESH
F32 = jnp.float32
BF16 = jnp.bfloat16
HIGHEST = lax.Precision.HIGHEST
EPSILON = 1e-05
LOWEST = -1e30
KEY_TILE = 512
ROWS = 256
TAIL = 16


def nt(a, b, precision=None):
    return lax.dot_general(
        a, b, (((1,), (1,)), ((), ())), preferred_element_type=F32, precision=precision
    )


def nn(a, b, precision=None):
    return lax.dot_general(
        a, b, (((1,), (0,)), ((), ())), preferred_element_type=F32, precision=precision
    )


def silu(a):
    return a / (1.0 + jnp.exp(-a))


def two_parts(value):
    high = value.astype(BF16)
    low = (value - high.astype(F32)).astype(BF16)
    return high, low


def kernel(
    dims,
    x_ref,
    gate_ref,
    b_ref,
    c_ref,
    step_ref,
    bias_ref,
    rate_ref,
    skip_ref,
    wx_ref,
    wb_ref,
    wc_ref,
    gain_ref,
    q_ref,
    k_ref,
    v_ref,
    mixer_ref,
    attn_ref,
    tail_x,
    tail_b,
    tail_c,
    pad_x,
    pad_s,
    signal,
    scaled,
    entry_decay,
    skip_rows,
    b_turned,
    b_held,
    c_held,
    log_held,
    logt_held,
    state_out,
    decay_out,
    state_in,
    decay_in,
    prefix,
    total_out,
    total_decay_out,
    total_in,
    total_decay_in,
    enter_out,
    enter_in,
    diagonal,
    gated,
    squares,
    kv,
    q_far,
    q_rows,
    o_far,
    o_in,
    m_held,
    acc_held,
    tail_send,
    tail_recv,
    pair_send,
    pair_recv,
    ring_send,
    ring_recv,
    row_send,
    row_recv,
    a2a_send,
    a2a_recv,
    tot_send,
    tot_recv,
    back_send,
    back_recv,
    sq_send,
    sq_recv,
):
    Y, Z, TP = dims
    T = x_ref.shape[0]
    HW = x_ref.shape[1]
    heads = HW // P_SIZE
    W = HW // Z
    G = b_ref.shape[1] // STATE
    GW = HW // G
    YZ = Y * Z
    QW = q_ref.shape[1] // 2
    grouped = QW // HD

    x = lax.axis_index("seq_0")
    y = lax.axis_index("seq_1")
    z = lax.axis_index("seq_2")
    t = lax.axis_index("tp")
    seq = x * YZ + y * Z + z
    count = 2 * YZ

    def place(index):
        return (index // YZ, (index // Z) % Y, index % Z, t)

    after = place((seq + 1) % count)
    before = place((seq + count - 1) % count)
    partner = (1 - x, Y - 1 - y, z, t)

    def z_peer(d):
        return (x, y, (z + d) % Z, t)

    def y_peer(d):
        return (x, (y + d) % Y, z, t)

    group = x * Y + y

    def group_peer(d):
        other = (group + d) % (2 * Y)
        return (other // Y, other % Y, z, t)

    def tp_peer(d):
        return (x, y, z, (t + d) % TP)

    barrier = pltpu.get_barrier_semaphore()
    greeted = [after, before]
    greeted += [z_peer(d) for d in range(1, Z)]
    greeted += [group_peer(d) for d in range(1, 2 * Y)]
    greeted += [tp_peer(d) for d in range(1, TP)]
    for peer in greeted:
        pl.semaphore_signal(barrier, inc=1, device_id=peer, device_id_type=MESH)

    def remote(src, dst, send, recv, peer):
        return pltpu.make_async_remote_copy(
            src_ref=src,
            dst_ref=dst,
            send_sem=send,
            recv_sem=recv,
            device_id=peer,
            device_id_type=MESH,
        )

    sent = []

    def start(src, dst, send, recv, peer):
        copy = remote(src, dst, send, recv, peer)
        copy.start()
        sent.append(copy)

    def arrived(dst, send, recv, peer):
        remote(dst, dst, send, recv, peer).wait_recv()

    def block_of(half, yy, zz):
        if half == 0:
            return x * YZ + yy * Z + zz
        return (1 - x) * YZ + (Y - 1 - yy) * Z + zz

    def kv_at(half, yy, zz):
        return kv.at[:, pl.ds(pl.multiple_of(block_of(half, yy, zz) * T, T), T), :]

    own_rows = pl.ds(pl.multiple_of(block_of(0, y, z) * T, T), T)
    kv[0, own_rows, :] = k_ref[:, pl.ds(pl.multiple_of(x * HD, HD), HD)]
    kv[1, own_rows, :] = v_ref[:, pl.ds(pl.multiple_of(x * HD, HD), HD)]
    for h in range(grouped):
        q_rows[0, h * T : (h + 1) * T, :] = q_ref[
            :, pl.ds(pl.multiple_of(x * QW + h * HD, HD), HD)
        ]

    step_in = step_ref[...] + bias_ref[...]
    step = jnp.maximum(step_in, 0.0) + jnp.log(1.0 + jnp.exp(-jnp.abs(step_in)))
    rows_at = lax.broadcasted_iota(jnp.int32, (T, T), 0)
    cols_at = lax.broadcasted_iota(jnp.int32, (T, T), 1)
    lower = jnp.where(rows_at >= cols_at, 1.0, 0.0).astype(F32)
    wide = jnp.concatenate(
        [-step * rate_ref[...], jnp.zeros((T, STATE - heads), F32)], axis=1
    )
    log_decay = nn(lower, wide, HIGHEST)
    log_held[...] = log_decay
    logt_held[...] = log_decay.T
    log_decay = log_decay[:, :heads]
    last = log_decay[T - 1 : T, :]
    closing = jnp.exp(last - log_decay)
    columns = jnp.concatenate([step, step * closing, jnp.exp(log_decay)], axis=0)
    columns_high, columns_low = two_parts(columns)
    whole = jnp.concatenate(
        [
            jnp.broadcast_to(jnp.exp(last), (8, heads)),
            jnp.broadcast_to(skip_ref[...], (8, heads)),
        ],
        axis=0,
    )
    whole_high, whole_low = two_parts(whole)

    pl.semaphore_wait(barrier, len(greeted))

    start(x_ref.at[T - TAIL :, :], tail_x, tail_send.at[0], tail_recv.at[0], after)
    start(b_ref.at[T - TAIL :, :], tail_b, tail_send.at[1], tail_recv.at[1], after)
    start(c_ref.at[T - TAIL :, :], tail_c, tail_send.at[2], tail_recv.at[2], after)
    far_cols = pl.ds(pl.multiple_of((1 - x) * HD, HD), HD)
    for i, ref in enumerate((k_ref, v_ref)):
        start(
            ref.at[:, far_cols],
            kv.at[i, own_rows, :],
            pair_send.at[i],
            pair_recv.at[i],
            partner,
        )

    right_steps = Z // 2
    left_steps = (Z - 1) // 2

    def ring_start(half, s):
        if s < right_steps:
            piece = kv_at(half, y, (z + Z - s) % Z)
            start(piece, piece, ring_send.at[half, 0, s], ring_recv.at[half, 0, s], z_peer(1))
        if s < left_steps:
            piece = kv_at(half, y, (z + s) % Z)
            start(piece, piece, ring_send.at[half, 1, s], ring_recv.at[half, 1, s], z_peer(Z - 1))

    def ring_wait(half, s):
        if s < right_steps:
            piece = kv_at(half, y, (z + Z - 1 - s) % Z)
            arrived(piece, ring_send.at[half, 0, s], ring_recv.at[half, 0, s], z_peer(Z - 1))
        if s < left_steps:
            piece = kv_at(half, y, (z + 1 + s) % Z)
            arrived(piece, ring_send.at[half, 1, s], ring_recv.at[half, 1, s], z_peer(1))

    def row_start(half, d):
        piece = kv_at(half, y, (z + d) % Z)
        if Y > 1:
            start(piece, piece, row_send.at[half, 0, d], row_recv.at[half, 0, d], y_peer(1))
        if Y > 2:
            start(piece, piece, row_send.at[half, 1, d], row_recv.at[half, 1, d], y_peer(Y - 1))

    def row_forward(half, d):
        if Y > 1:
            piece = kv_at(half, (y + Y - 1) % Y, (z + d) % Z)
            arrived(piece, row_send.at[half, 0, d], row_recv.at[half, 0, d], y_peer(Y - 1))
            if Y > 3 and 2 * d < Z:
                start(piece, piece, row_send.at[half, 2, d], row_recv.at[half, 2, d], y_peer(1))
        if Y > 2:
            piece = kv_at(half, (y + 1) % Y, (z + d) % Z)
            arrived(piece, row_send.at[half, 1, d], row_recv.at[half, 1, d], y_peer(1))
            if Y > 3 and 2 * d >= Z:
                start(
                    piece, piece, row_send.at[half, 2, d], row_recv.at[half, 2, d], y_peer(Y - 1)
                )

    def row_last(half, d):
        if Y > 3:
            piece = kv_at(half, (y + 2) % Y, (z + d) % Z)
            arrived(
                piece,
                row_send.at[half, 2, d],
                row_recv.at[half, 2, d],
                y_peer(Y - 1 if 2 * d < Z else 1),
            )

    def offsets(s):
        found = []
        if s < right_steps:
            found.append(Z - 1 - s)
        if s < left_steps:
            found.append(1 + s)
        return found

    ring_start(0, 0)
    row_start(0, 0)
    start(
        q_ref.at[:, pl.ds(pl.multiple_of((1 - x) * QW, QW), QW)],
        q_far,
        pair_send.at[2],
        pair_recv.at[2],
        partner,
    )

    arrived(tail_x, tail_send.at[0], tail_recv.at[0], before)
    arrived(tail_b, tail_send.at[1], tail_recv.at[1], before)
    arrived(tail_c, tail_send.at[2], tail_recv.at[2], before)
    inside = jnp.where(seq > 0, 1.0, 0.0).astype(F32)

    def conv_silu(pad, tail, rows, weights):
        pad[0:8, :] = tail[8:16, :].astype(F32) * inside
        pad[8 : T + 8, :] = rows.astype(F32)
        total = weights[0:1, :] * pad[5 : T + 5, :]
        for k in range(1, CONV):
            total = total + weights[k : k + 1, :] * pad[5 + k : T + 5 + k, :]
        return silu(total)

    for g in range(G):
        cols = slice(g * STATE, (g + 1) * STATE)
        b_now = conv_silu(pad_s, tail_b[:, cols], b_ref[:, cols], wb_ref[:, cols])
        b_held[g] = b_now.astype(BF16)
        b_turned[g] = b_now.T.astype(BF16)
        c_now = conv_silu(pad_s, tail_c[:, cols], c_ref[:, cols], wc_ref[:, cols])
        c_held[g] = c_now.astype(BF16)

    for d in [*range(1, Z), 0]:
        k = (z + d) % Z
        at = pl.ds(pl.multiple_of(k * W, W), W)
        spread = jnp.where(
            lax.broadcasted_iota(jnp.int32, (heads, W), 0)
            == k * (W // P_SIZE) + lax.broadcasted_iota(jnp.int32, (heads, W), 1) // P_SIZE,
            1.0,
            0.0,
        ).astype(BF16)
        per_lane = nn(columns_high, spread) + nn(columns_low, spread)
        per_whole = nn(whole_high, spread) + nn(whole_low, spread)
        now = conv_silu(pad_x, tail_x[:, at], x_ref[:, at], wx_ref[:, at])
        signal[:, at] = now
        scaled[:, at] = (now * per_lane[:T]).astype(BF16)
        entry_decay[:, at] = per_lane[2 * T :]
        skip_rows[:, at] = per_whole[8:]
        weighted = (now * per_lane[T : 2 * T]).astype(BF16)
        state = nn(b_turned[k * W // GW], weighted)
        if d:
            state_out[d] = state.astype(BF16)
            decay_out[d] = per_whole[:8]
            start(state_out.at[d], state_in.at[z], a2a_send.at[0, d], a2a_recv.at[0, d], z_peer(d))
            start(decay_out.at[d], decay_in.at[z], a2a_send.at[1, d], a2a_recv.at[1, d], z_peer(d))
        else:
            state_in[z] = state.astype(BF16)
            decay_in[z] = per_whole[:8]

    for i in range(2):
        arrived(
            kv.at[i, pl.ds(pl.multiple_of(block_of(1, y, z) * T, T), T), :],
            pair_send.at[i],
            pair_recv.at[i],
            partner,
        )
    ring_start(1, 0)
    row_start(1, 0)

    causal = rows_at >= cols_at
    couplings = [nt(c_held[g], b_held[g]) for g in range(G)]
    lane_at = lax.broadcasted_iota(jnp.int32, (T, 2 * P_SIZE), 1)

    def pair_of_heads(p):
        mixes = []
        for h in (2 * p, 2 * p + 1):
            spread = log_held[:, h : h + 1] - logt_held[h : h + 1, :]
            decays = jnp.exp(jnp.where(causal, spread, LOWEST))
            mixes.append((decays * couplings[h * P_SIZE // GW]).astype(BF16))
        two = scaled[:, p * 128 : (p + 1) * 128]
        zero = jnp.zeros_like(two)
        stacked = jnp.concatenate(
            [jnp.where(lane_at < P_SIZE, two, zero), jnp.where(lane_at < P_SIZE, zero, two)],
            axis=0,
        )
        diagonal[:, p * 128 : (p + 1) * 128] = nn(jnp.concatenate(mixes, axis=1), stacked)

    pairs = heads // 2
    steps = max(right_steps, 1)
    for s in range(steps):
        for p in range(s * pairs // steps, (s + 1) * pairs // steps):
            pair_of_heads(p)
        for half in range(2):
            if s < right_steps:
                ring_wait(half, s)
                if s + 1 < right_steps:
                    ring_start(half, s + 1)
                for d in offsets(s):
                    row_start(half, d)

    for d in range(1, Z):
        source = (z + Z - d) % Z
        arrived(state_in.at[source], a2a_send.at[0, d], a2a_recv.at[0, d], z_peer(Z - d))
        arrived(decay_in.at[source], a2a_send.at[1, d], a2a_recv.at[1, d], z_peer(Z - d))
    running = jnp.zeros((STATE, W), F32)
    running_decay = jnp.ones((8, W), F32)
    for i in range(Z):
        prefix[i] = running
        keep = decay_in[i]
        running = running * keep[0:1] + state_in[i].astype(F32)
        running_decay = running_decay * keep
    total_out[...] = running.astype(BF16)
    total_decay_out[...] = running_decay
    total_in[group] = running.astype(BF16)
    total_decay_in[group] = running_decay
    for d in range(1, 2 * Y):
        start(total_out, total_in.at[group], tot_send.at[0, d], tot_recv.at[0, d], group_peer(d))
        start(
            total_decay_out,
            total_decay_in.at[group],
            tot_send.at[1, d],
            tot_recv.at[1, d],
            group_peer(d),
        )

    for d in range(Z):
        for half in range(2):
            row_forward(half, d)

    for d in range(1, 2 * Y):
        source = (group + 2 * Y - d) % (2 * Y)
        arrived(total_in.at[source], tot_send.at[0, d], tot_recv.at[0, d], group_peer(2 * Y - d))
        arrived(
            total_decay_in.at[source], tot_send.at[1, d], tot_recv.at[1, d], group_peer(2 * Y - d)
        )
    entering = jnp.zeros((STATE, W), F32)
    for i in range(2 * Y):
        further = entering * total_decay_in[i][0:1] + total_in[i].astype(F32)
        entering = jnp.where(i < group, further, entering)
    so_far = jnp.ones((8, W), F32)
    for i in range(Z):
        enter_out[i] = (prefix[i] + entering * so_far[0:1]).astype(BF16)
        so_far = so_far * decay_in[i]
    for d in range(1, Z):
        k = (z + d) % Z
        start(enter_out.at[k], enter_in.at[z], back_send.at[d], back_recv.at[d], z_peer(d))
    enter_in[z] = enter_out[z]

    for d in range(Z):
        for half in range(2):
            row_last(half, d)
    arrived(q_far, pair_send.at[2], pair_recv.at[2], partner)
    for h in range(grouped):
        q_rows[1, h * T : (h + 1) * T, :] = q_far[:, h * HD : (h + 1) * HD]

    scale = math.log2(math.e) / math.sqrt(HD)
    all_rows = grouped * T
    chunk = min(ROWS, all_rows)

    def attend(which, position):
        m_held[...] = jnp.full(m_held.shape, LOWEST, F32)
        acc_held[...] = jnp.zeros(acc_held.shape, F32)

        def tile(index, masked):
            keys_at = pl.ds(pl.multiple_of(index * KEY_TILE, KEY_TILE), KEY_TILE)
            keys = kv[0, keys_at, :]
            values = jnp.concatenate([kv[1, keys_at, :], jnp.ones((KEY_TILE, HD), BF16)], axis=1)
            for r in range(0, all_rows, chunk):
                scores = nt(q_rows[which, r : r + chunk, :], keys)
                if masked:
                    row = lax.broadcasted_iota(jnp.int32, (chunk, KEY_TILE), 0) % T
                    col = lax.broadcasted_iota(jnp.int32, (chunk, KEY_TILE), 1)
                    scores = jnp.where(
                        col + index * KEY_TILE <= row + position * T, scores, LOWEST
                    )
                old = m_held[r : r + chunk, :]
                new = jnp.maximum(old, jnp.max(scores, axis=1, keepdims=True))
                m_held[r : r + chunk, :] = new
                factor = jnp.exp2((old - new) * scale)
                weights = jnp.concatenate(
                    [
                        jnp.exp2((scores[:, j : j + HD] - new) * scale).astype(BF16)
                        for j in range(0, KEY_TILE, HD)
                    ],
                    axis=1,
                )
                product = nn(weights, values)
                acc_held[r : r + chunk, :] = (
                    acc_held[r : r + chunk, :] * jnp.concatenate([factor, factor], axis=1)
                    + product
                )

        full = position * T // KEY_TILE
        lax.fori_loop(0, full, lambda i, n: (tile(i, False), n)[1], 0)
        tile(full, True)

    def result(h):
        both = acc_held[h * T : (h + 1) * T, :]
        return (both[:, :HD] / both[:, HD:]).astype(BF16)

    attend(1, block_of(1, y, z))
    for h in range(grouped):
        o_far[:, h * HD : (h + 1) * HD] = result(h)
    start(o_far, o_in, pair_send.at[3], pair_recv.at[3], partner)
    attend(0, seq)
    for h in range(grouped):
        attn_ref[:, pl.ds(pl.multiple_of(x * QW + h * HD, HD), HD)] = result(h)

    for d in range(1, Z):
        source = (z + Z - d) % Z
        arrived(enter_in.at[source], back_send.at[d], back_recv.at[d], z_peer(Z - d))
    summed = jnp.zeros((T, 128), F32)
    for k in range(Z):
        cols = slice(k * W, (k + 1) * W)
        off = nn(c_held[k * W // GW], enter_in[k])
        mixed = diagonal[:, cols] + entry_decay[:, cols] * off
        mixed = mixed + skip_rows[0:1, cols] * signal[:, cols]
        now = mixed * silu(gate_ref[:, cols].astype(F32))
        gated[:, cols] = now
        now = now * now
        for j in range(0, W, 128):
            summed = summed + now[:, j : j + 128]
    squares[t] = nt(jnp.ones((8, 128), F32), summed, HIGHEST)
    for d in range(1, TP):
        start(squares.at[t], squares.at[t], sq_send.at[d], sq_recv.at[d], tp_peer(d))
    for d in range(1, TP):
        source = (t + TP - d) % TP
        arrived(squares.at[source], sq_send.at[d], sq_recv.at[d], tp_peer(TP - d))
    everything = squares[0]
    for i in range(1, TP):
        everything = everything + squares[i]
    everything = jnp.broadcast_to(everything[0:1, :], (T, T)).T
    factor = lax.rsqrt(everything / (HW * TP) + EPSILON)
    for j in range(0, HW, 128):
        mixer_ref[:, j : j + 128] = (
            gated[:, j : j + 128] * factor * gain_ref[:, j : j + 128]
        ).astype(BF16)

    arrived(o_in, pair_send.at[3], pair_recv.at[3], partner)
    attn_ref[:, pl.ds(pl.multiple_of((1 - x) * QW, QW), QW)] = o_in[...]
    for copy in sent:
        copy.wait_send()


def shards(dims, *args):
    (x, gate, b, c, step, bias, rate, skip, wx, wb, wc, gain, q, k, v) = args
    bias, rate, skip, gain = (a.reshape(1, -1) for a in (bias, rate, skip, gain))
    Y, Z, TP = dims
    T, HW = x.shape
    W = HW // Z
    G = b.shape[1] // STATE
    count = 2 * Y * Z
    QW = q.shape[1] // 2
    rows = QW // HD * T
    vmem, dma = pltpu.VMEM, pltpu.SemaphoreType.DMA
    scratch = [
        vmem((TAIL, HW), BF16),
        vmem((TAIL, G * STATE), BF16),
        vmem((TAIL, G * STATE), BF16),
        vmem((T + 8, W), F32),
        vmem((T + 8, STATE), F32),
        vmem((T, HW), F32),
        vmem((T, HW), BF16),
        vmem((T, HW), F32),
        vmem((8, HW), F32),
        vmem((G, STATE, T), BF16),
        vmem((G, T, STATE), BF16),
        vmem((G, T, STATE), BF16),
        vmem((T, STATE), F32),
        vmem((STATE, T), F32),
        vmem((Z, STATE, W), BF16),
        vmem((Z, 8, W), F32),
        vmem((Z, STATE, W), BF16),
        vmem((Z, 8, W), F32),
        vmem((Z, STATE, W), F32),
        vmem((STATE, W), BF16),
        vmem((8, W), F32),
        vmem((2 * Y, STATE, W), BF16),
        vmem((2 * Y, 8, W), F32),
        vmem((Z, STATE, W), BF16),
        vmem((Z, STATE, W), BF16),
        vmem((T, HW), F32),
        vmem((T, HW), F32),
        vmem((TP, 8, 128), F32),
        vmem((2, count * T, HD), BF16),
        vmem((T, QW), BF16),
        vmem((2, rows, HD), BF16),
        vmem((T, QW), BF16),
        vmem((T, QW), BF16),
        vmem((rows, HD), F32),
        vmem((rows, 2 * HD), F32),
        dma((3,)),
        dma((3,)),
        dma((4,)),
        dma((4,)),
        dma((2, 2, max(Z // 2, 1))),
        dma((2, 2, max(Z // 2, 1))),
        dma((2, 3, Z)),
        dma((2, 3, Z)),
        dma((2, Z)),
        dma((2, Z)),
        dma((2, 2 * Y)),
        dma((2, 2 * Y)),
        dma((Z,)),
        dma((Z,)),
        dma((TP,)),
        dma((TP,)),
    ]
    whole = pl.BlockSpec(memory_space=pltpu.VMEM)
    return pl.pallas_call(
        functools.partial(kernel, dims),
        out_shape=(
            jax.ShapeDtypeStruct((T, HW), BF16),
            jax.ShapeDtypeStruct((T, 2 * QW), BF16),
        ),
        in_specs=[whole] * 15,
        out_specs=(whole, whole),
        scratch_shapes=scratch,
        compiler_params=pltpu.CompilerParams(
            collective_id=0, has_side_effects=True, vmem_limit_bytes=60 * 1024 * 1024
        ),
        name="hybrid",
    )(x, gate, b, c, step, bias, rate, skip, wx, wb, wc, gain, q, k, v)


def build(mesh, Y, Z):
    TP = mesh.shape["tp"]
    torus = Mesh(mesh.devices.reshape(2, Y, Z, TP), (*SEQ, "tp"))
    cut, by_tp = P(SEQ, "tp"), P("tp")
    taps = P(None, "tp")
    placed = (cut,) * 5 + (by_tp,) * 3 + (taps,) * 3 + (by_tp,) + (cut,) * 3
    return jax.shard_map(
        functools.partial(shards, (Y, Z, TP)),
        mesh=torus,
        in_specs=placed,
        out_specs=(cut, cut),
        check_vma=False,
    )


def solution(mesh):
    return build(mesh, 4, 8)
```

time: 489 us -> 98 us (0.20)
  waiting for transfers between devices: 232 us -> 0 us
  Pallas kernels: 0 us -> 93 us
  starting transfers between devices: 66.1 us -> 0 us
  matrix products: 65.1 us -> 0 us
  blocking collectives: 37 us -> 0 us
  other arithmetic: 33.9 us -> 0 us
  local copies, waits for them, and re-layouts: 36 us -> 4.18 us
  between operations: 14.6 us -> 0.65 us
    all_gather x4 -> x0, waiting for transfers between devices: 176 us -> none  [the longest x1 93.2 us: in_one_piece(): lax.all_gather(both, axis, axis=dim, tiled=True)]
    pallas_call x0 -> x1, Pallas kernels: none -> 93 us  [shards(): pl.pallas_call(functools.partial(kernel, dims), out_shape=(jax.ShapeDtype...]
    dot_general x39 -> x0, matrix products: 65.1 us -> none  [the longest x17 43.9 us: attend_update(): jnp.einsum('hgqk,khd->hgqd', rounded, value_three, preferred_element_type...]
    ppermute x15 -> x0, waiting for transfers between devices: 55 us -> none  [the longest x12 55 us: partner(): return lax.ppermute(block, axis, route)]
    ppermute x15 -> x0, starting transfers between devices: 54.2 us -> none  [the longest x12 44 us: partner(): return lax.ppermute(block, axis, route)]
    all_gather x3 -> x0, blocking collectives: 37 us -> none  [entering_2(): pieces = jax.tree.map(lambda part: lax.all_gather(part, axis), subtotal)]
    dynamic_slice x16 -> x0, local copies, waits for them, and re-layouts: 17 us -> none  [visit(): lax.dynamic_slice_in_dim(value_piece, position * span, span, 0)]
    reduce_sum x19 -> x0, other arithmetic: 12.2 us -> none  [the longest x17 11.7 us: attend_update(): totals = totals * factor + jnp.sum(probs, axis=-1)]
  transfers between devices with their start and end apart: 20 -> 0, of which waited for: 11 -> 0; matrix products, arithmetic and copies ran while one was open for 26% -> 0% of each run, Pallas kernels for 0% -> 0%
where the time goes in v1:
time: 98 us; the launch traced here: 97.8 us
  Pallas kernels  93 us (95%)
  local copies, waits for them, and re-layouts  4.18 us (4%)
    pallas_call x1, Pallas kernels, shards(): pl.pallas_call(functools.partial(kernel, dims), out_shape=(jax.ShapeDtype...  93 us
    unnamed x5, local copies, waits for them, and re-layouts  4.18 us

profile of v1, /device:TPU:1, one launch (start us, length us, event | category | flops | bytes accessed | tf_op | source)
XLA Modules:
  0.0 97.8 jit_solution(11879593268613729784)
XLA Ops:
  0.6 1.4 %copy.17.step_ref = f32[128,32]{1,0:T(8,128)} copy(f32[128,32]{0,1:T(8,128)} %param.19) | data formatting | bytes 32768 | tf_op args[4]
  2.1 93.0 %hybrid.1 = (bf16[128,2048]{1,0:T(8,128)(2,1)}, bf16[128,2048]{1,0:T(8,128)(2,1)}) custom-call(bf16[128,2048]{1,0:T(8,128)(2,1)} %x_ref.1, bf16[128,2048]{1,0:T(8,128)(2,1)} %gate_ref.1, bf16[128,256]{1,0:T(8,128)(2,1)} %b_ref.1, bf16[128,256]{1,0:T(8,128)(2,1)} %c_ref.1, f32[128,32]{1,0:T(8,128)} %copy.17.step_ref, f32[1,32]{1,0:T(1,128)} %bitcast.5, ...), custom_call_target="tpu_custom_call" | custom-call | tf_op jit(solution)/shard_map/hybrid/pallas_call | solution.py:611
  95.1 0.0 copy-start
  95.1 1.9 %copy.20 = bf16[128,2048]{1,0:T(8,128)(2,1)} copy(bf16[128,2048]{1,0:T(8,128)(2,1)} %get-tuple-element.4) | data formatting | bytes 1048576
  97.0 0.0 copy-done
  97.0 0.8 copy.21
Async XLA Ops:
  95.1 2.0 %copy-start = (bf16[128,2048]{1,0:T(8,128)(2,1)S(1)}, bf16[128,2048]{1,0:T(8,128)(2,1)}, u32[]{:S(2)}) copy-start(bf16[128,2048]{1,0:T(8,128)(2,1)} %get-tuple-element.5) | copy-start | bytes 1572868

commit v2 on v1

--- a/solution.py
+++ b/solution.py
@@ -202,7 +202,10 @@
             :, pl.ds(pl.multiple_of(x * QW + h * HD, HD), HD)
         ]
 
-    step_in = step_ref[...] + bias_ref[...]
+    turned = jnp.concatenate(
+        [step_ref[...], jnp.zeros((STATE - heads, T), F32)], axis=0
+    ).T
+    step_in = turned[:, :heads] + bias_ref[...]
     step = jnp.maximum(step_in, 0.0) + jnp.log(1.0 + jnp.exp(-jnp.abs(step_in)))
     rows_at = lax.broadcasted_iota(jnp.int32, (T, T), 0)
     cols_at = lax.broadcasted_iota(jnp.int32, (T, T), 1)
@@ -331,7 +334,40 @@
         c_now = conv_silu(pad_s, tail_c[:, cols], c_ref[:, cols], wc_ref[:, cols])
         c_held[g] = c_now.astype(BF16)
 
-    for d in [*range(1, Z), 0]:
+    HALF = W // 2
+    chunks = W // 128
+
+    def pack(row):
+        parts = [row[:, i * 128 : (i + 1) * 128] for i in range(chunks)]
+        if chunks < 8:
+            parts.append(jnp.ones((8 - chunks, 128), F32))
+        return jnp.concatenate(parts, axis=0)
+
+    def unpack(packed, half):
+        return jnp.concatenate(
+            [packed[i : i + 1] for i in range(half * chunks // 2, (half + 1) * chunks // 2)], axis=1
+        )
+
+    def advance(half, s):
+        if s < right_steps:
+            ring_wait(half, s)
+            if s + 1 < right_steps:
+                ring_start(half, s + 1)
+            for d in offsets(s):
+                row_start(half, d)
+
+    def pair_arrives():
+        for i in range(2):
+            arrived(
+                kv.at[i, pl.ds(pl.multiple_of(block_of(1, y, z) * T, T), T), :],
+                pair_send.at[i],
+                pair_recv.at[i],
+                partner,
+            )
+        ring_start(1, 0)
+        row_start(1, 0)
+
+    def slice_of_heads(d):
         k = (z + d) % Z
         at = pl.ds(pl.multiple_of(k * W, W), W)
         spread = jnp.where(
@@ -348,25 +384,38 @@
         entry_decay[:, at] = per_lane[2 * T :]
         skip_rows[:, at] = per_whole[8:]
         weighted = (now * per_lane[T : 2 * T]).astype(BF16)
-        state = nn(b_turned[k * W // GW], weighted)
+        state = nn(b_turned[k * W // GW], weighted).astype(BF16)
+        packed = pack(per_whole[0:1])
         if d:
-            state_out[d] = state.astype(BF16)
-            decay_out[d] = per_whole[:8]
-            start(state_out.at[d], state_in.at[z], a2a_send.at[0, d], a2a_recv.at[0, d], z_peer(d))
-            start(decay_out.at[d], decay_in.at[z], a2a_send.at[1, d], a2a_recv.at[1, d], z_peer(d))
+            decay_out[d] = packed
+            for half in range(2):
+                state_out[half, d] = state[:, half * HALF : (half + 1) * HALF]
+            start(decay_out.at[d], decay_in.at[z], a2a_send.at[2, d], a2a_recv.at[2, d], z_peer(d))
+            start_state(0, d)
         else:
-            state_in[z] = state.astype(BF16)
-            decay_in[z] = per_whole[:8]
-
-    for i in range(2):
-        arrived(
-            kv.at[i, pl.ds(pl.multiple_of(block_of(1, y, z) * T, T), T), :],
-            pair_send.at[i],
-            pair_recv.at[i],
-            partner,
+            decay_in[z] = packed
+            for half in range(2):
+                state_in[half, z] = state[:, half * HALF : (half + 1) * HALF]
+
+    def start_state(half, d):
+        start(
+            state_out.at[half, d],
+            state_in.at[half, z],
+            a2a_send.at[half, d],
+            a2a_recv.at[half, d],
+            z_peer(d),
         )
-    ring_start(1, 0)
-    row_start(1, 0)
+
+    todo = [lambda: advance(0, 0), pair_arrives, lambda: advance(1, 0), lambda: advance(0, 1)]
+    order = [*range(1, Z), 0]
+    for i, d in enumerate(order):
+        slice_of_heads(d)
+        if i % 2 and todo:
+            todo.pop(0)()
+    for d in range(1, Z):
+        start_state(1, d)
+    for act in todo:
+        act()
 
     causal = rows_at >= cols_at
     couplings = [nt(c_held[g], b_held[g]) for g in range(G)]
@@ -387,133 +436,188 @@
         diagonal[:, p * 128 : (p + 1) * 128] = nn(jnp.concatenate(mixes, axis=1), stacked)
 
     pairs = heads // 2
-    steps = max(right_steps, 1)
-    for s in range(steps):
-        for p in range(s * pairs // steps, (s + 1) * pairs // steps):
-            pair_of_heads(p)
-        for half in range(2):
-            if s < right_steps:
-                ring_wait(half, s)
-                if s + 1 < right_steps:
-                    ring_start(half, s + 1)
-                for d in offsets(s):
-                    row_start(half, d)
+    todo = []
+    for n in range(1, right_steps):
+        todo.append(lambda n=n: advance(1, n))
+        if n + 1 < right_steps:
+            todo.append(lambda n=n: advance(0, n + 1))
+    for p in range(pairs):
+        pair_of_heads(p)
+        if p % 3 == 2 and todo:
+            todo.pop(0)()
+    for act in todo:
+        act()
 
     for d in range(1, Z):
         source = (z + Z - d) % Z
-        arrived(state_in.at[source], a2a_send.at[0, d], a2a_recv.at[0, d], z_peer(Z - d))
-        arrived(decay_in.at[source], a2a_send.at[1, d], a2a_recv.at[1, d], z_peer(Z - d))
-    running = jnp.zeros((STATE, W), F32)
-    running_decay = jnp.ones((8, W), F32)
+        arrived(decay_in.at[source], a2a_send.at[2, d], a2a_recv.at[2, d], z_peer(Z - d))
+    running_decay = jnp.ones((8, 128), F32)
     for i in range(Z):
-        prefix[i] = running
-        keep = decay_in[i]
-        running = running * keep[0:1] + state_in[i].astype(F32)
-        running_decay = running_decay * keep
-    total_out[...] = running.astype(BF16)
+        running_decay = running_decay * decay_in[i]
     total_decay_out[...] = running_decay
-    total_in[group] = running.astype(BF16)
     total_decay_in[group] = running_decay
     for d in range(1, 2 * Y):
-        start(total_out, total_in.at[group], tot_send.at[0, d], tot_recv.at[0, d], group_peer(d))
         start(
             total_decay_out,
             total_decay_in.at[group],
-            tot_send.at[1, d],
-            tot_recv.at[1, d],
+            tot_send.at[2, d],
+            tot_recv.at[2, d],
             group_peer(d),
         )
 
-    for d in range(Z):
+    def scan(half):
+        for d in range(1, Z):
+            source = (z + Z - d) % Z
+            arrived(
+                state_in.at[half, source], a2a_send.at[half, d], a2a_recv.at[half, d], z_peer(Z - d)
+            )
+        running = jnp.zeros((STATE, HALF), F32)
+        for i in range(Z):
+            prefix[half, i] = running
+            running = running * unpack(decay_in[i], half) + state_in[half, i].astype(F32)
+        total_out[half] = running.astype(BF16)
+        total_in[half, group] = running.astype(BF16)
+        for d in range(1, 2 * Y):
+            start(
+                total_out.at[half],
+                total_in.at[half, group],
+                tot_send.at[half, d],
+                tot_recv.at[half, d],
+                group_peer(d),
+            )
+
+    def enter(half):
+        for d in range(1, 2 * Y):
+            source = (group + 2 * Y - d) % (2 * Y)
+            back = group_peer(2 * Y - d)
+            if half == 0:
+                arrived(total_decay_in.at[source], tot_send.at[2, d], tot_recv.at[2, d], back)
+            arrived(total_in.at[half, source], tot_send.at[half, d], tot_recv.at[half, d], back)
+        entering = jnp.zeros((STATE, HALF), F32)
+        for i in range(2 * Y):
+            further = entering * unpack(total_decay_in[i], half) + total_in[half, i].astype(F32)
+            entering = jnp.where(i < group, further, entering)
+        so_far = jnp.ones((8, 128), F32)
+        for i in range(Z):
+            enter_out[half, i] = (prefix[half, i] + entering * unpack(so_far, half)).astype(BF16)
+            so_far = so_far * decay_in[i]
+        for d in range(1, Z):
+            k = (z + d) % Z
+            start(
+                enter_out.at[half, k],
+                enter_in.at[half, z],
+                back_send.at[half, d],
+                back_recv.at[half, d],
+                z_peer(d),
+            )
+        enter_in[half, z] = enter_out[half, z]
+
+    piece_order = [0]
+    for n in range(right_steps):
+        piece_order += offsets(n)
+    scale = math.log2(math.e) / math.sqrt(HD)
+    all_rows = grouped * T
+    chunk = min(ROWS, all_rows)
+
+    key_tile = min(KEY_TILE, Z * T)
+    m_held[...] = jnp.full(m_held.shape, LOWEST, F32)
+    acc_held[...] = jnp.zeros(acc_held.shape, F32)
+
+    def tile(which, start_key, position, masked):
+        keys_at = pl.ds(pl.multiple_of(start_key, key_tile), key_tile)
+        keys = kv[0, keys_at, :]
+        values = jnp.concatenate([kv[1, keys_at, :], jnp.ones((key_tile, HD), BF16)], axis=1)
+        for r in range(0, all_rows, chunk):
+            scores = nt(q_rows[which, r : r + chunk, :], keys)
+            if masked:
+                row = lax.broadcasted_iota(jnp.int32, (chunk, key_tile), 0) % T
+                col = lax.broadcasted_iota(jnp.int32, (chunk, key_tile), 1)
+                scores = jnp.where(col + start_key <= row + position * T, scores, LOWEST)
+            old = m_held[which, r : r + chunk, :]
+            new = jnp.maximum(old, jnp.max(scores, axis=1, keepdims=True))
+            m_held[which, r : r + chunk, :] = new
+            factor = jnp.exp2((old - new) * scale)
+            weights = jnp.concatenate(
+                [
+                    jnp.exp2((scores[:, j : j + HD] - new) * scale).astype(BF16)
+                    for j in range(0, key_tile, HD)
+                ],
+                axis=1,
+            )
+            product = nn(weights, values)
+            acc_held[which, r : r + chunk, :] = (
+                acc_held[which, r : r + chunk, :] * jnp.concatenate([factor, factor], axis=1)
+                + product
+            )
+
+    def attend(rows):
+        def one(i, carry):
+            which, half, at = i // 2 % 2, i % 2, i // 4
+            yy = rows[0] if len(rows) == 1 else rows[0] * (1 - at) + rows[1] * at
+            position = (1 - which) * seq + which * block_of(1, y, z)
+            first = (1 - half) * block_of(0, yy, 0) + half * block_of(1, yy, 0)
+            inside_row = jnp.minimum(jnp.maximum(position - first, 0), Z)
+            full = inside_row * T // key_tile
+
+            def body(n, c):
+                tile(which, first * T + n * key_tile, position, False)
+                return c
+
+            lax.fori_loop(0, full, body, 0)
+
+            @pl.when((position >= first) & (position < first + Z))
+            def _():
+                tile(which, first * T + full * key_tile, position, True)
+
+            return carry
+
+        lax.fori_loop(0, 4 * len(rows), one, 0)
+
+    scan(0)
+    scan(1)
+    arrived(q_far, pair_send.at[2], pair_recv.at[2], partner)
+    for h in range(grouped):
+        q_rows[1, h * T : (h + 1) * T, :] = q_far[:, h * HD : (h + 1) * HD]
+    for d in piece_order[: Z // 2]:
         for half in range(2):
             row_forward(half, d)
-
-    for d in range(1, 2 * Y):
-        source = (group + 2 * Y - d) % (2 * Y)
-        arrived(total_in.at[source], tot_send.at[0, d], tot_recv.at[0, d], group_peer(2 * Y - d))
-        arrived(
-            total_decay_in.at[source], tot_send.at[1, d], tot_recv.at[1, d], group_peer(2 * Y - d)
-        )
-    entering = jnp.zeros((STATE, W), F32)
-    for i in range(2 * Y):
-        further = entering * total_decay_in[i][0:1] + total_in[i].astype(F32)
-        entering = jnp.where(i < group, further, entering)
-    so_far = jnp.ones((8, W), F32)
-    for i in range(Z):
-        enter_out[i] = (prefix[i] + entering * so_far[0:1]).astype(BF16)
-        so_far = so_far * decay_in[i]
-    for d in range(1, Z):
-        k = (z + d) % Z
-        start(enter_out.at[k], enter_in.at[z], back_send.at[d], back_recv.at[d], z_peer(d))
-    enter_in[z] = enter_out[z]
-
+    attend([y])
+    enter(0)
+    for d in piece_order[Z // 2 :]:
+        for half in range(2):
+            row_forward(half, d)
+    enter(1)
+    if Y == 2:
+        attend([(y + 1) % Y])
+    if Y > 2:
+        attend([(y + Y - 1) % Y, (y + 1) % Y])
     for d in range(Z):
         for half in range(2):
             row_last(half, d)
-    arrived(q_far, pair_send.at[2], pair_recv.at[2], partner)
+    if Y > 3:
+        attend([(y + 2) % Y])
+
+    def result(which, h):
+        both = acc_held[which, h * T : (h + 1) * T, :]
+        return (both[:, :HD] / both[:, HD:]).astype(BF16)
+
     for h in range(grouped):
-        q_rows[1, h * T : (h + 1) * T, :] = q_far[:, h * HD : (h + 1) * HD]
-
-    scale = math.log2(math.e) / math.sqrt(HD)
-    all_rows = grouped * T
-    chunk = min(ROWS, all_rows)
-
-    def attend(which, position):
-        m_held[...] = jnp.full(m_held.shape, LOWEST, F32)
-        acc_held[...] = jnp.zeros(acc_held.shape, F32)
-
-        def tile(index, masked):
-            keys_at = pl.ds(pl.multiple_of(index * KEY_TILE, KEY_TILE), KEY_TILE)
-            keys = kv[0, keys_at, :]
-            values = jnp.concatenate([kv[1, keys_at, :], jnp.ones((KEY_TILE, HD), BF16)], axis=1)
-            for r in range(0, all_rows, chunk):
-                scores = nt(q_rows[which, r : r + chunk, :], keys)
-                if masked:
-                    row = lax.broadcasted_iota(jnp.int32, (chunk, KEY_TILE), 0) % T
-                    col = lax.broadcasted_iota(jnp.int32, (chunk, KEY_TILE), 1)
-                    scores = jnp.where(
-                        col + index * KEY_TILE <= row + position * T, scores, LOWEST
-                    )
-                old = m_held[r : r + chunk, :]
-                new = jnp.maximum(old, jnp.max(scores, axis=1, keepdims=True))
-                m_held[r : r + chunk, :] = new
-                factor = jnp.exp2((old - new) * scale)
-                weights = jnp.concatenate(
-                    [
-                        jnp.exp2((scores[:, j : j + HD] - new) * scale).astype(BF16)
-                        for j in range(0, KEY_TILE, HD)
-                    ],
-                    axis=1,
-                )
-                product = nn(weights, values)
-                acc_held[r : r + chunk, :] = (
-                    acc_held[r : r + chunk, :] * jnp.concatenate([factor, factor], axis=1)
-                    + product
-                )
-
-        full = position * T // KEY_TILE
-        lax.fori_loop(0, full, lambda i, n: (tile(i, False), n)[1], 0)
-        tile(full, True)
-
-    def result(h):
-        both = acc_held[h * T : (h + 1) * T, :]
-        return (both[:, :HD] / both[:, HD:]).astype(BF16)
-
-    attend(1, block_of(1, y, z))
+        o_far[:, h * HD : (h + 1) * HD] = result(1, h)
+    start(o_far, o_in, pair_send.at[3], pair_recv.at[3], partner)
     for h in range(grouped):
-        o_far[:, h * HD : (h + 1) * HD] = result(h)
-    start(o_far, o_in, pair_send.at[3], pair_recv.at[3], partner)
-    attend(0, seq)
-    for h in range(grouped):
-        attn_ref[:, pl.ds(pl.multiple_of(x * QW + h * HD, HD), HD)] = result(h)
+        attn_ref[:, pl.ds(pl.multiple_of(x * QW + h * HD, HD), HD)] = result(0, h)
 
     for d in range(1, Z):
         source = (z + Z - d) % Z
-        arrived(enter_in.at[source], back_send.at[d], back_recv.at[d], z_peer(Z - d))
+        for half in range(2):
+            arrived(
+                enter_in.at[half, source], back_send.at[half, d], back_recv.at[half, d], z_peer(Z - d)
+            )
     summed = jnp.zeros((T, 128), F32)
     for k in range(Z):
         cols = slice(k * W, (k + 1) * W)
-        off = nn(c_held[k * W // GW], enter_in[k])
+        entry = jnp.concatenate([enter_in[0, k], enter_in[1, k]], axis=1)
+        off = nn(c_held[k * W // GW], entry)
         mixed = diagonal[:, cols] + entry_decay[:, cols] * off
         mixed = mixed + skip_rows[0:1, cols] * signal[:, cols]
         now = mixed * silu(gate_ref[:, cols].astype(F32))
@@ -569,17 +673,17 @@
         vmem((G, T, STATE), BF16),
         vmem((T, STATE), F32),
         vmem((STATE, T), F32),
-        vmem((Z, STATE, W), BF16),
-        vmem((Z, 8, W), F32),
-        vmem((Z, STATE, W), BF16),
-        vmem((Z, 8, W), F32),
-        vmem((Z, STATE, W), F32),
-        vmem((STATE, W), BF16),
-        vmem((8, W), F32),
-        vmem((2 * Y, STATE, W), BF16),
-        vmem((2 * Y, 8, W), F32),
-        vmem((Z, STATE, W), BF16),
-        vmem((Z, STATE, W), BF16),
+        vmem((2, Z, STATE, W // 2), BF16),
+        vmem((Z, 8, 128), F32),
+        vmem((2, Z, STATE, W // 2), BF16),
+        vmem((Z, 8, 128), F32),
+        vmem((2, Z, STATE, W // 2), F32),
+        vmem((2, STATE, W // 2), BF16),
+        vmem((8, 128), F32),
+        vmem((2, 2 * Y, STATE, W // 2), BF16),
+        vmem((2 * Y, 8, 128), F32),
+        vmem((2, Z, STATE, W // 2), BF16),
+        vmem((2, Z, STATE, W // 2), BF16),
         vmem((T, HW), F32),
         vmem((T, HW), F32),
         vmem((TP, 8, 128), F32),
@@ -588,8 +692,8 @@
         vmem((2, rows, HD), BF16),
         vmem((T, QW), BF16),
         vmem((T, QW), BF16),
-        vmem((rows, HD), F32),
-        vmem((rows, 2 * HD), F32),
+        vmem((2, rows, HD), F32),
+        vmem((2, rows, 2 * HD), F32),
         dma((3,)),
         dma((3,)),
         dma((4,)),
@@ -598,12 +702,12 @@
         dma((2, 2, max(Z // 2, 1))),
         dma((2, 3, Z)),
         dma((2, 3, Z)),
+        dma((3, Z)),
+        dma((3, Z)),
+        dma((3, 2 * Y)),
+        dma((3, 2 * Y)),
         dma((2, Z)),
         dma((2, Z)),
-        dma((2, 2 * Y)),
-        dma((2, 2 * Y)),
-        dma((Z,)),
-        dma((Z,)),
         dma((TP,)),
         dma((TP,)),
     ]
@@ -621,7 +725,7 @@
             collective_id=0, has_side_effects=True, vmem_limit_bytes=60 * 1024 * 1024
         ),
         name="hybrid",
-    )(x, gate, b, c, step, bias, rate, skip, wx, wb, wc, gain, q, k, v)
+    )(x, gate, b, c, step.T, bias, rate, skip, wx, wb, wc, gain, q, k, v)
 
 
 def build(mesh, Y, Z):

time: 98 us -> 81 us (0.83)
  Pallas kernels: 93 us -> 77.2 us
  local copies, waits for them, and re-layouts: 4.18 us -> 2.74 us
    pallas_call x1, Pallas kernels: 93 us -> 77.2 us  [shards(): pl.pallas_call(functools.partial(kernel, dims), out_shape=(jax.ShapeDtype...]
    unnamed x5 -> x4, local copies, waits for them, and re-layouts: 4.18 us -> 2.74 us
where the time goes in v2:
time: 81 us; the launch traced here: 80.6 us
  Pallas kernels  77.2 us (95%)
  local copies, waits for them, and re-layouts  2.74 us (3%)
    pallas_call x1, Pallas kernels, shards(): pl.pallas_call(functools.partial(kernel, dims), out_shape=(jax.ShapeDtype...  77.2 us
    unnamed x4, local copies, waits for them, and re-layouts  2.74 us

profile of v2, /device:TPU:1, one launch (start us, length us, event | category | flops | bytes accessed | tf_op | source)
XLA Modules:
  0.0 80.6 jit_solution(6278974135451270770)
XLA Ops:
  0.6 77.2 %hybrid.1 = (bf16[128,2048]{1,0:T(8,128)(2,1)}, bf16[128,2048]{1,0:T(8,128)(2,1)}) custom-call(bf16[128,2048]{1,0:T(8,128)(2,1)} %x_ref.1, bf16[128,2048]{1,0:T(8,128)(2,1)} %gate_ref.1, bf16[128,256]{1,0:T(8,128)(2,1)} %b_ref.1, bf16[128,256]{1,0:T(8,128)(2,1)} %c_ref.1, f32[32,128]{1,0:T(8,128)} %bitcast.5, f32[1,32]{1,0:T(1,128)} %bitcast.7, ...), custom_call_target="tpu_custom_call" | custom-call | tf_op jit(solution)/shard_map/hybrid/pallas_call | solution.py:715
  77.8 0.0 copy-start
  77.9 1.9 %copy.19 = bf16[128,2048]{1,0:T(8,128)(2,1)} copy(bf16[128,2048]{1,0:T(8,128)(2,1)} %get-tuple-element.4) | data formatting | bytes 1048576
  79.8 0.0 copy-done
  79.8 0.8 copy.20
Async XLA Ops:
  77.8 2.0 %copy-start = (bf16[128,2048]{1,0:T(8,128)(2,1)S(1)}, bf16[128,2048]{1,0:T(8,128)(2,1)}, u32[]{:S(2)}) copy-start(bf16[128,2048]{1,0:T(8,128)(2,1)} %get-tuple-element.5) | copy-start | bytes 1572868

commit v3 on v2

v3 whole, which is shorter than its diff:
```python
import functools
import math

import jax
import jax.numpy as jnp
from jax import lax
from jax.experimental import pallas as pl
from jax.experimental.pallas import tpu as pltpu
from jax.sharding import Mesh
from jax.sharding import PartitionSpec as P

P_SIZE = 64
STATE = 128
HD = 128
CONV = 4
SEQ = ("seq_0", "seq_1", "seq_2")
MESH = pl.DeviceIdType.MESH
F32 = jnp.float32
BF16 = jnp.bfloat16
HIGHEST = lax.Precision.HIGHEST
EPSILON = 1e-05
LOWEST = -1e30
KEY_TILE = 512
ROWS = 256
TAIL = 16


def nt(a, b, precision=None):
    return lax.dot_general(
        a, b, (((1,), (1,)), ((), ())), preferred_element_type=F32, precision=precision
    )


def nn(a, b, precision=None):
    return lax.dot_general(
        a, b, (((1,), (0,)), ((), ())), preferred_element_type=F32, precision=precision
    )


def silu(a):
    return a / (1.0 + jnp.exp(-a))


def two_parts(value):
    high = value.astype(BF16)
    low = (value - high.astype(F32)).astype(BF16)
    return high, low


def kernel(
    dims,
    x_far,
    gate_far,
    b_far,
    c_far,
    step_ref,
    bias_ref,
    rate_ref,
    skip_ref,
    wx_ref,
    wb_ref,
    wc_ref,
    gain_ref,
    q_far_in,
    k_far,
    v_far,
    mixer_ref,
    attn_ref,
    x_ref,
    gate_ref,
    b_ref,
    c_ref,
    q_ref,
    k_ref,
    v_ref,
    load_sems,
    tail_x,
    tail_b,
    tail_c,
    pad_x,
    pad_s,
    b_first,
    c_first,
    weighted,
    early_step,
    early_close,
    whole_decay,
    signal,
    scaled,
    entry_decay,
    skip_rows,
    b_turned,
    b_held,
    c_held,
    log_held,
    logt_held,
    state_out,
    decay_out,
    state_in,
    decay_in,
    prefix,
    total_out,
    total_decay_out,
    total_in,
    total_decay_in,
    enter_out,
    enter_in,
    diagonal,
    gated,
    squares,
    kv,
    q_far,
    q_rows,
    o_far,
    o_in,
    m_held,
    acc_held,
    tail_send,
    tail_recv,
    pair_send,
    pair_recv,
    ring_send,
    ring_recv,
    row_send,
    row_recv,
    a2a_send,
    a2a_recv,
    tot_send,
    tot_recv,
    back_send,
    back_recv,
    sq_send,
    sq_recv,
):
    Y, Z, TP = dims
    T = x_ref.shape[0]
    HW = x_ref.shape[1]
    heads = HW // P_SIZE
    W = HW // Z
    G = b_ref.shape[1] // STATE
    GW = HW // G
    YZ = Y * Z
    QW = q_ref.shape[1] // 2
    grouped = QW // HD

    x = lax.axis_index("seq_0")
    y = lax.axis_index("seq_1")
    z = lax.axis_index("seq_2")
    t = lax.axis_index("tp")
    seq = x * YZ + y * Z + z
    count = 2 * YZ

    def place(index):
        return (index // YZ, (index // Z) % Y, index % Z, t)

    after = place((seq + 1) % count)
    before = place((seq + count - 1) % count)

    core = t % 2
    high = y // (Y // 2)
    own_slot = (core + high) % 2 == 0
    facing = Y - 1 - y
    beside = y + 1 - 2 * (y % 2)
    sibling = (x, y, z, t + 1 - 2 * core)

    def z_peer(d):
        return (x, y, (z + d) % Z, t)

    y_peer = (x, beside, z, t)

    group = x * Y + y

    def group_peer(d):
        other = (group + d) % (2 * Y)
        return (other // Y, other % Y, z, t)

    def tp_peer(d):
        return (x, y, z, (t + d) % TP)

    total_in[...] = jnp.zeros(total_in.shape, BF16)
    total_decay_in[...] = jnp.ones(total_decay_in.shape, F32)
    barrier = pltpu.get_barrier_semaphore()
    greeted = [after, before]
    greeted += [z_peer(d) for d in range(1, Z)]
    greeted += [group_peer(d) for d in range(1, 2 * Y)]
    greeted += [tp_peer(d) for d in range(1, TP)]
    greeted += [(1 - x, y, z, t + 1 - 2 * core), (x, facing, z, t + 1 - 2 * core)]
    for peer in greeted:
        pl.semaphore_signal(barrier, inc=1, device_id=peer, device_id_type=MESH)

    def remote(src, dst, send, recv, peer):
        return pltpu.make_async_remote_copy(
            src_ref=src,
            dst_ref=dst,
            send_sem=send,
            recv_sem=recv,
            device_id=peer,
            device_id_type=MESH,
        )

    sent = []
    inside = jnp.where(seq > 0, 1.0, 0.0).astype(F32)
    far = (x_far, b_far, c_far, k_far, v_far, q_far_in, gate_far)
    held = (x_ref, b_ref, c_ref, k_ref, v_ref, q_ref, gate_ref)
    loads = [
        pltpu.make_async_copy(src, dst, load_sems.at[i]) for i, (src, dst) in enumerate(zip(far, held))
    ]
    for load in loads:
        load.start()

    def start(src, dst, send, recv, peer):
        copy = remote(src, dst, send, recv, peer)
        copy.start()
        sent.append(copy)

    def arrived(dst, send, recv, peer):
        remote(dst, dst, send, recv, peer).wait_recv()

    def block_of(slot, sharer, other, zz):
        xx = (x + core + sharer + high + slot) % 2
        low = facing * high + y * (1 - high)
        low = low * (1 - other) + (Y // 2 - 1 - low) * other
        up = (high + slot) % 2
        return xx * YZ + (low * (1 - up) + (Y - 1 - low) * up) * Z + zz

    def kv_at(slot, sharer, other, zz):
        first = pl.multiple_of(block_of(slot, sharer, other, zz) * T, T)
        return kv.at[:, pl.ds(first, T), :]

    own_rows = pl.ds(pl.multiple_of(seq * T, T), T)

    turned = jnp.concatenate(
        [step_ref[...], jnp.zeros((STATE - heads, T), F32)], axis=0
    ).T
    step_in = turned[:, :heads] + bias_ref[...]
    step = jnp.maximum(step_in, 0.0) + jnp.log(1.0 + jnp.exp(-jnp.abs(step_in)))
    rows_at = lax.broadcasted_iota(jnp.int32, (T, T), 0)
    cols_at = lax.broadcasted_iota(jnp.int32, (T, T), 1)
    lower = jnp.where(rows_at >= cols_at, 1.0, 0.0).astype(F32)
    wide = jnp.concatenate(
        [-step * rate_ref[...], jnp.zeros((T, STATE - heads), F32)], axis=1
    )
    log_decay = nn(lower, wide, HIGHEST)
    log_held[...] = log_decay
    logt_held[...] = log_decay.T
    log_decay = log_decay[:, :heads]
    last = log_decay[T - 1 : T, :]
    closing = jnp.exp(last - log_decay)
    columns = jnp.concatenate([step, step * closing, jnp.exp(log_decay)], axis=0)
    columns_high, columns_low = two_parts(columns)
    whole = jnp.concatenate(
        [
            jnp.broadcast_to(jnp.exp(last), (8, heads)),
            jnp.broadcast_to(skip_ref[...], (8, heads)),
        ],
        axis=0,
    )
    whole_high, whole_low = two_parts(whole)

    def conv_silu(pad, tail, rows, weights):
        count = rows.shape[0]
        if tail is None:
            pad[0:8, :] = jnp.zeros((8, rows.shape[1]), F32)
        else:
            pad[0:8, :] = tail[8:16, :].astype(F32) * inside
        pad[8 : count + 8, :] = rows.astype(F32)
        total = weights[0:1, :] * pad[5 : count + 5, :]
        for k in range(1, CONV):
            total = total + weights[k : k + 1, :] * pad[5 + k : count + 5 + k, :]
        return silu(total)

    for load in loads[:-1]:
        load.wait()

    @pl.when(own_slot)
    def _():
        kv[0, own_rows, :] = k_ref[:, pl.ds(pl.multiple_of(x * HD, HD), HD)]
        kv[1, own_rows, :] = v_ref[:, pl.ds(pl.multiple_of(x * HD, HD), HD)]
        for h in range(grouped):
            q_rows[0, h * T : (h + 1) * T, :] = q_ref[
                :, pl.ds(pl.multiple_of(x * QW + h * HD, HD), HD)
            ]

    pl.semaphore_wait(barrier, len(greeted))

    start(x_ref.at[T - TAIL :, :], tail_x, tail_send.at[0], tail_recv.at[0], after)
    start(b_ref.at[T - TAIL :, :], tail_b, tail_send.at[1], tail_recv.at[1], after)
    start(c_ref.at[T - TAIL :, :], tail_c, tail_send.at[2], tail_recv.at[2], after)
    across = (1 - x, y, z, t + 1 - 2 * core)
    face = (x, facing, z, t + 1 - 2 * core)
    corner = (1 - x, facing, z, t)

    def kv_columns(j):
        return pl.ds(pl.multiple_of(j * HD, HD), HD)

    def q_columns(j):
        return pl.ds(pl.multiple_of(j * QW, QW), QW)

    def pair_copies(what):
        found = []
        for condition, j, slot, peer in (
            (own_slot, 1 - x, 0, across),
            (~own_slot, x, 1, face),
            (~own_slot, 1 - x, 1, corner),
        ):
            n = len(found)
            if what == 2:
                copy = remote(
                    q_ref.at[:, q_columns(j)], q_far.at[slot], pair_send.at[2, n],
                    pair_recv.at[2, slot], peer,
                )
            else:
                copy = remote(
                    (k_ref, v_ref)[what].at[:, kv_columns(j)], kv.at[what, own_rows, :],
                    pair_send.at[what, n], pair_recv.at[what, slot], peer,
                )
            found.append((condition, copy))
        return found

    def back_copies():
        found = []
        for condition, slot, peer in (
            (~own_slot, 0, across),
            (~own_slot, 1, face),
            (own_slot, 1, corner),
        ):
            found.append(
                (
                    condition,
                    remote(
                        o_far.at[slot], o_in.at[x], pair_send.at[3, len(found)],
                        pair_recv.at[3, x], peer,
                    ),
                )
            )
        return found

    def start_all(pieces):
        for condition, copy in pieces:
            pl.when(condition)(copy.start)

    quad = [pair_copies(0), pair_copies(1)]
    for pieces in quad:
        start_all(pieces)

    right_steps = Z // 2
    left_steps = (Z - 1) // 2

    def ring_start(slot, s):
        if s < right_steps:
            piece = kv_at(slot, 0, 0, (z + Z - s) % Z)
            start(piece, piece, ring_send.at[slot, 0, s], ring_recv.at[slot, 0, s], z_peer(1))
        if s < left_steps:
            piece = kv_at(slot, 0, 0, (z + s) % Z)
            start(piece, piece, ring_send.at[slot, 1, s], ring_recv.at[slot, 1, s], z_peer(Z - 1))

    def ring_wait(slot, s):
        if s < right_steps:
            piece = kv_at(slot, 0, 0, (z + Z - 1 - s) % Z)
            arrived(piece, ring_send.at[slot, 0, s], ring_recv.at[slot, 0, s], z_peer(Z - 1))
        if s < left_steps:
            piece = kv_at(slot, 0, 0, (z + 1 + s) % Z)
            arrived(piece, ring_send.at[slot, 1, s], ring_recv.at[slot, 1, s], z_peer(1))

    def row_start(slot, d):
        piece = kv_at(slot, 0, 0, (z + d) % Z)
        start(piece, piece, row_send.at[slot, 0, d], row_recv.at[slot, 0, d], y_peer)
        start(piece, piece, row_send.at[slot, 1, d], row_recv.at[slot, 1, d], sibling)

    def near_arrives(slot, d):
        piece = kv_at(slot, 1, 0, (z + d) % Z)
        arrived(piece, row_send.at[slot, 1, d], row_recv.at[slot, 1, d], sibling)

    def row_forward(slot, d):
        piece = kv_at(slot, 0, 1, (z + d) % Z)
        arrived(piece, row_send.at[slot, 0, d], row_recv.at[slot, 0, d], y_peer)
        start(piece, piece, row_send.at[slot, 2, d], row_recv.at[slot, 2, d], sibling)

    def row_last(slot, d):
        piece = kv_at(slot, 1, 1, (z + d) % Z)
        arrived(piece, row_send.at[slot, 2, d], row_recv.at[slot, 2, d], sibling)

    def offsets(s):
        found = []
        if s < right_steps:
            found.append(Z - 1 - s)
        if s < left_steps:
            found.append(1 + s)
        return found

    quad.append(pair_copies(2))
    start_all(quad[2])

    def pair_arrives(slot):
        def wait():
            for i in range(2):
                place = block_of(slot, 0, 0, z)
                arrived(
                    kv.at[i, pl.ds(pl.multiple_of(place * T, T), T), :],
                    pair_send.at[i, 0],
                    pair_recv.at[i, slot],
                    across,
                )

        if slot == 0:
            pl.when(~own_slot)(wait)
        else:
            wait()
        ring_start(slot, 0)
        row_start(slot, 0)

    b_first[...] = conv_silu(pad_s, None, b_ref[...], wb_ref)
    c_first[...] = conv_silu(pad_s, None, c_ref[...], wc_ref)
    for k in range(Z):
        at = slice(k * W, (k + 1) * W)
        spread = jnp.where(
            lax.broadcasted_iota(jnp.int32, (heads, W), 0)
            == k * (W // P_SIZE) + lax.broadcasted_iota(jnp.int32, (heads, W), 1) // P_SIZE,
            1.0,
            0.0,
        ).astype(BF16)
        per_lane = nn(columns_high, spread) + nn(columns_low, spread)
        per_whole = nn(whole_high, spread) + nn(whole_low, spread)
        now = conv_silu(pad_x, None, x_ref[:, at], wx_ref[:, at])
        signal[:, at] = now
        scaled[:, at] = (now * per_lane[:T]).astype(BF16)
        weighted[:, at] = (now * per_lane[T : 2 * T]).astype(BF16)
        early_step[:, at] = per_lane[:TAIL]
        early_close[:, at] = per_lane[T : T + TAIL]
        entry_decay[:, at] = per_lane[2 * T :]
        skip_rows[:, at] = per_whole[8:]
        whole_decay[:, at] = per_whole[:8]


    arrived(tail_x, tail_send.at[0], tail_recv.at[0], before)
    arrived(tail_b, tail_send.at[1], tail_recv.at[1], before)
    arrived(tail_c, tail_send.at[2], tail_recv.at[2], before)
    b_first[:TAIL, :] = conv_silu(pad_s, tail_b, b_ref[:TAIL, :], wb_ref)
    c_first[:TAIL, :] = conv_silu(pad_s, tail_c, c_ref[:TAIL, :], wc_ref)
    for g in range(G):
        cols = slice(g * STATE, (g + 1) * STATE)
        b_held[g] = b_first[:, cols].astype(BF16)
        b_turned[g] = b_first[:, cols].T.astype(BF16)
        c_held[g] = c_first[:, cols].astype(BF16)
    for k in range(Z):
        at = slice(k * W, (k + 1) * W)
        now = conv_silu(pad_x, tail_x[:, at], x_ref[:TAIL, at], wx_ref[:, at])
        signal[:TAIL, at] = now
        scaled[:TAIL, at] = (now * early_step[:, at]).astype(BF16)
        weighted[:TAIL, at] = (now * early_close[:, at]).astype(BF16)
    pair_arrives(0)
    pair_arrives(1)

    HALF = W // 2
    chunks = W // 128

    def pack(row):
        parts = [row[:, i * 128 : (i + 1) * 128] for i in range(chunks)]
        if chunks < 8:
            parts.append(jnp.ones((8 - chunks, 128), F32))
        return jnp.concatenate(parts, axis=0)

    def unpack(packed, half):
        return jnp.concatenate(
            [packed[i : i + 1] for i in range(half * chunks // 2, (half + 1) * chunks // 2)], axis=1
        )

    def advance(half, s):
        if s < right_steps:
            ring_wait(half, s)
            if s + 1 < right_steps:
                ring_start(half, s + 1)
            for d in offsets(s):
                row_start(half, d)

    def slice_of_heads(d):
        k = (z + d) % Z
        at = pl.ds(pl.multiple_of(k * W, W), W)
        state = nn(b_turned[k * W // GW], weighted[:, at]).astype(BF16)
        packed = pack(whole_decay[0:1, at])
        if d:
            decay_out[d] = packed
            for half in range(2):
                state_out[half, d] = state[:, half * HALF : (half + 1) * HALF]
            start(decay_out.at[d], decay_in.at[z], a2a_send.at[2, d], a2a_recv.at[2, d], z_peer(d))
        else:
            decay_in[z] = packed
            for half in range(2):
                state_in[half, z] = state[:, half * HALF : (half + 1) * HALF]

    def start_state(half, d):
        start(
            state_out.at[half, d],
            state_in.at[half, z],
            a2a_send.at[half, d],
            a2a_recv.at[half, d],
            z_peer(d),
        )

    for d in [*range(1, Z), 0]:
        slice_of_heads(d)

    causal = rows_at >= cols_at
    couplings = [nt(c_held[g], b_held[g]) for g in range(G)]
    lane_at = lax.broadcasted_iota(jnp.int32, (T, 2 * P_SIZE), 1)

    def pair_of_heads(p):
        mixes = []
        for h in (2 * p, 2 * p + 1):
            spread = log_held[:, h : h + 1] - logt_held[h : h + 1, :]
            decays = jnp.exp(jnp.where(causal, spread, LOWEST))
            mixes.append((decays * couplings[h * P_SIZE // GW]).astype(BF16))
        two = scaled[:, p * 128 : (p + 1) * 128]
        zero = jnp.zeros_like(two)
        stacked = jnp.concatenate(
            [jnp.where(lane_at < P_SIZE, two, zero), jnp.where(lane_at < P_SIZE, zero, two)],
            axis=0,
        )
        diagonal[:, p * 128 : (p + 1) * 128] = nn(jnp.concatenate(mixes, axis=1), stacked)

    pairs = heads // 2

    def some_pairs(low, high):
        for p in range(low * pairs // 16, high * pairs // 16):
            pair_of_heads(p)

    def ring_step(s):
        for slot in range(2):
            advance(slot, s)

    for d in range(1, Z):
        source = (z + Z - d) % Z
        arrived(decay_in.at[source], a2a_send.at[2, d], a2a_recv.at[2, d], z_peer(Z - d))
    running_decay = jnp.ones((8, 128), F32)
    for i in range(Z):
        running_decay = running_decay * decay_in[i]
    total_decay_out[...] = running_decay
    total_decay_in[group] = running_decay
    totals_sent = []

    def total_start(src, dst, kind, d):
        copy = remote(src, dst, tot_send.at[kind, d], tot_recv.at[kind, d], group_peer(d))
        later = group + d < 2 * Y
        pl.when(later)(copy.start)
        totals_sent.append((later, copy))

    def total_arrived(dst, kind, d):
        @pl.when(group >= d)
        def _():
            arrived(dst, tot_send.at[kind, d], tot_recv.at[kind, d], group_peer(2 * Y - d))

    for d in range(1, 2 * Y):
        total_start(total_decay_out, total_decay_in.at[group], 2, d)

    def scan(half):
        for d in range(1, Z):
            source = (z + Z - d) % Z
            arrived(
                state_in.at[half, source], a2a_send.at[half, d], a2a_recv.at[half, d], z_peer(Z - d)
            )
        running = jnp.zeros((STATE, HALF), F32)
        for i in range(Z):
            prefix[half, i] = running
            running = running * unpack(decay_in[i], half) + state_in[half, i].astype(F32)
        total_out[half] = running.astype(BF16)
        total_in[half, group] = running.astype(BF16)
        for d in range(1, 2 * Y):
            total_start(total_out.at[half], total_in.at[half, group], half, d)

    def enter(half):
        for d in range(1, 2 * Y):
            source = (group + 2 * Y - d) % (2 * Y)
            if half == 0:
                total_arrived(total_decay_in.at[source], 2, d)
            total_arrived(total_in.at[half, source], half, d)
        entering = jnp.zeros((STATE, HALF), F32)
        for i in range(2 * Y):
            further = entering * unpack(total_decay_in[i], half) + total_in[half, i].astype(F32)
            entering = jnp.where(i < group, further, entering)
        so_far = jnp.ones((8, 128), F32)
        for i in range(Z):
            enter_out[half, i] = (prefix[half, i] + entering * unpack(so_far, half)).astype(BF16)
            so_far = so_far * decay_in[i]
        for d in range(1, Z):
            k = (z + d) % Z
            start(
                enter_out.at[half, k],
                enter_in.at[half, z],
                back_send.at[half, d],
                back_recv.at[half, d],
                z_peer(d),
            )
        enter_in[half, z] = enter_out[half, z]

    piece_order = [0]
    for n in range(right_steps):
        piece_order += offsets(n)
    scale = math.log2(math.e) / math.sqrt(HD)
    all_rows = grouped * T
    chunk = min(ROWS, all_rows)

    span = max(Z // 2, 1)
    key_tile = span * T
    m_held[...] = jnp.full(m_held.shape, LOWEST, F32)
    acc_held[...] = jnp.zeros(acc_held.shape, F32)

    def tile(which, start_key, position, masked):
        keys_at = pl.ds(pl.multiple_of(start_key, key_tile), key_tile)
        keys = kv[0, keys_at, :]
        values = jnp.concatenate([kv[1, keys_at, :], jnp.ones((key_tile, HD), BF16)], axis=1)
        for r in range(0, all_rows, chunk):
            scores = nt(q_rows[which, r : r + chunk, :], keys)
            if masked:
                row = lax.broadcasted_iota(jnp.int32, (chunk, key_tile), 0) % T
                col = lax.broadcasted_iota(jnp.int32, (chunk, key_tile), 1)
                scores = jnp.where(col + start_key <= row + position * T, scores, LOWEST)
            old = m_held[which, r : r + chunk, :]
            new = jnp.maximum(old, jnp.max(scores, axis=1, keepdims=True))
            m_held[which, r : r + chunk, :] = new
            factor = jnp.exp2((old - new) * scale)
            weights = jnp.concatenate(
                [
                    jnp.exp2((scores[:, j : j + HD] - new) * scale).astype(BF16)
                    for j in range(0, key_tile, HD)
                ],
                axis=1,
            )
            product = nn(weights, values)
            acc_held[which, r : r + chunk, :] = (
                acc_held[which, r : r + chunk, :] * jnp.concatenate([factor, factor], axis=1)
                + product
            )

    def attend(other, which, parts):
        near = z // span

        def one(i, carry):
            n = (near + parts[0] + i // 4) % 2
            sharer, slot = i // 2 % 2, i % 2
            position = block_of(which, 0, 0, z)
            first = block_of(slot, sharer, other, 0) + n * span

            @pl.when(first + span <= position)
            def _():
                tile(which, first * T, position, False)

            @pl.when((first <= position) & (position < first + span))
            def _():
                tile(which, first * T, position, True)

            return carry

        lax.fori_loop(0, 4 * len(parts), one, 0)

    def unroll_queries(slot):
        arrived(q_far.at[slot], pair_send.at[2, 0], pair_recv.at[2, slot], across)
        for h in range(grouped):
            q_rows[slot, h * T : (h + 1) * T, :] = q_far[slot, :, h * HD : (h + 1) * HD]

    def result(which, h):
        both = acc_held[which, h * T : (h + 1) * T, :]
        return (both[:, :HD] / both[:, HD:]).astype(BF16)

    def results_leave(slot):
        for h in range(grouped):
            o_far[slot, :, h * HD : (h + 1) * HD] = result(slot, h)
        start_all(returned[slot])

    returned = back_copies()
    returned = [returned[:1], returned[1:]]

    def forward(pieces):
        for d in pieces:
            for slot in range(2):
                row_forward(slot, d)

    far_first = sorted(range(1, Z), key=lambda d: -min(d, Z - d))
    first, second = far_first[: Z // 2], far_first[Z // 2 :]

    def states(half, which):
        for d in which:
            start_state(half, d)

    def near(pieces):
        for d in pieces:
            for slot in range(2):
                near_arrives(slot, d)

    some_pairs(0, 8)
    ring_step(0)
    states(0, first)
    ring_step(1)
    states(0, second)
    ring_step(2)
    some_pairs(8, 16)
    states(1, first)
    states(1, second)
    pl.when(~own_slot)(lambda: unroll_queries(0))
    unroll_queries(1)
    near([d for d in piece_order if d != Z // 2])
    attend(0, 1, (0,))
    ring_step(3)
    near([Z // 2])
    attend(0, 0, (0,))
    scan(0)
    attend(0, 1, (1,))
    scan(1)
    attend(0, 0, (1,))
    enter(0)
    forward(piece_order)
    for d in piece_order:
        for slot in range(2):
            row_last(slot, d)
    enter(1)
    attend(1, 1, (0, 1))
    results_leave(1)
    attend(1, 0, (0, 1))
    results_leave(0)

    @pl.when(own_slot)
    def _():
        attn_ref[:, q_columns(x)] = o_far[0]

    for d in range(1, Z):
        source = (z + Z - d) % Z
        for half in range(2):
            arrived(
                enter_in.at[half, source], back_send.at[half, d], back_recv.at[half, d], z_peer(Z - d)
            )
    loads[-1].wait()
    summed = jnp.zeros((T, 128), F32)
    for k in range(Z):
        cols = slice(k * W, (k + 1) * W)
        entry = jnp.concatenate([enter_in[0, k], enter_in[1, k]], axis=1)
        off = nn(c_held[k * W // GW], entry)
        mixed = diagonal[:, cols] + entry_decay[:, cols] * off
        mixed = mixed + skip_rows[0:1, cols] * signal[:, cols]
        now = mixed * silu(gate_ref[:, cols].astype(F32))
        gated[:, cols] = now
        now = now * now
        for j in range(0, W, 128):
            summed = summed + now[:, j : j + 128]
    squares[t] = nt(jnp.ones((8, 128), F32), summed, HIGHEST)
    for d in range(1, TP):
        start(squares.at[t], squares.at[t], sq_send.at[d], sq_recv.at[d], tp_peer(d))
    for d in range(1, TP):
        source = (t + TP - d) % TP
        arrived(squares.at[source], sq_send.at[d], sq_recv.at[d], tp_peer(TP - d))
    everything = squares[0]
    for i in range(1, TP):
        everything = everything + squares[i]
    everything = jnp.broadcast_to(everything[0:1, :], (T, T)).T
    factor = lax.rsqrt(everything / (HW * TP) + EPSILON)
    for j in range(0, HW, 128):
        mixer_ref[:, j : j + 128] = (
            gated[:, j : j + 128] * factor * gain_ref[:, j : j + 128]
        ).astype(BF16)

    def results_arrive(j):
        arrived(o_in.at[j], pair_send.at[3, 0], pair_recv.at[3, j], across)
        attn_ref[:, q_columns(j)] = o_in[j]

    pl.when(~own_slot)(lambda: results_arrive(x))
    results_arrive(1 - x)
    for pieces in [*quad, *returned, totals_sent]:
        for condition, copy in pieces:
            pl.when(condition)(copy.wait_send)
    for copy in sent:
        copy.wait_send()


def shards(dims, *args):
    (x, gate, b, c, step, bias, rate, skip, wx, wb, wc, gain, q, k, v) = args
    bias, rate, skip, gain = (a.reshape(1, -1) for a in (bias, rate, skip, gain))
    Y, Z, TP = dims
    T, HW = x.shape
    W = HW // Z
    G = b.shape[1] // STATE
    count = 2 * Y * Z
    QW = q.shape[1] // 2
    rows = QW // HD * T
    vmem, dma = pltpu.VMEM, pltpu.SemaphoreType.DMA
    scratch = [
        *(vmem(a.shape, BF16) for a in (x, gate, b, c, q, k, v)),
        dma((7,)),
        vmem((TAIL, HW), BF16),
        vmem((TAIL, G * STATE), BF16),
        vmem((TAIL, G * STATE), BF16),
        vmem((T + 8, W), F32),
        vmem((T + 8, G * STATE), F32),
        vmem((T, G * STATE), F32),
        vmem((T, G * STATE), F32),
        vmem((T, HW), BF16),
        vmem((TAIL, HW), F32),
        vmem((TAIL, HW), F32),
        vmem((8, HW), F32),
        vmem((T, HW), F32),
        vmem((T, HW), BF16),
        vmem((T, HW), F32),
        vmem((8, HW), F32),
        vmem((G, STATE, T), BF16),
        vmem((G, T, STATE), BF16),
        vmem((G, T, STATE), BF16),
        vmem((T, STATE), F32),
        vmem((STATE, T), F32),
        vmem((2, Z, STATE, W // 2), BF16),
        vmem((Z, 8, 128), F32),
        vmem((2, Z, STATE, W // 2), BF16),
        vmem((Z, 8, 128), F32),
        vmem((2, Z, STATE, W // 2), F32),
        vmem((2, STATE, W // 2), BF16),
        vmem((8, 128), F32),
        vmem((2, 2 * Y, STATE, W // 2), BF16),
        vmem((2 * Y, 8, 128), F32),
        vmem((2, Z, STATE, W // 2), BF16),
        vmem((2, Z, STATE, W // 2), BF16),
        vmem((T, HW), F32),
        vmem((T, HW), F32),
        vmem((TP, 8, 128), F32),
        vmem((2, count * T, HD), BF16),
        vmem((2, T, QW), BF16),
        vmem((2, rows, HD), BF16),
        vmem((2, T, QW), BF16),
        vmem((2, T, QW), BF16),
        vmem((2, rows, HD), F32),
        vmem((2, rows, 2 * HD), F32),
        dma((3,)),
        dma((3,)),
        dma((4, 3)),
        dma((4, 2)),
        dma((2, 2, max(Z // 2, 1))),
        dma((2, 2, max(Z // 2, 1))),
        dma((2, 3, Z)),
        dma((2, 3, Z)),
        dma((3, Z)),
        dma((3, Z)),
        dma((3, 2 * Y)),
        dma((3, 2 * Y)),
        dma((2, Z)),
        dma((2, Z)),
        dma((TP,)),
        dma((TP,)),
    ]
    whole = pl.BlockSpec(memory_space=pltpu.VMEM)
    return pl.pallas_call(
        functools.partial(kernel, dims),
        out_shape=(
            jax.ShapeDtypeStruct((T, HW), BF16),
            jax.ShapeDtypeStruct((T, 2 * QW), BF16),
        ),
        in_specs=[
            pl.BlockSpec(memory_space=pl.ANY) if a.dtype == BF16 else whole for a in args
        ],
        out_specs=(whole, whole),
        scratch_shapes=scratch,
        compiler_params=pltpu.CompilerParams(
            collective_id=0, has_side_effects=True, vmem_limit_bytes=60 * 1024 * 1024
        ),
        name="hybrid",
    )(x, gate, b, c, step.T, bias, rate, skip, wx, wb, wc, gain, q, k, v)


def build(mesh, Y, Z):
    TP = mesh.shape["tp"]
    torus = Mesh(mesh.devices.reshape(2, Y, Z, TP), (*SEQ, "tp"))
    cut, by_tp = P(SEQ, "tp"), P("tp")
    taps = P(None, "tp")
    placed = (cut,) * 5 + (by_tp,) * 3 + (taps,) * 3 + (by_tp,) + (cut,) * 3
    return jax.shard_map(
        functools.partial(shards, (Y, Z, TP)),
        mesh=torus,
        in_specs=placed,
        out_specs=(cut, cut),
        check_vma=False,
    )


def solution(mesh):
    return build(mesh, 4, 8)
```

time: 81 us -> 76.5 us (0.944)
  Pallas kernels: 77.2 us -> 72.9 us
    pallas_call x1, Pallas kernels: 77.2 us -> 72.9 us  [shards(): pl.pallas_call(functools.partial(kernel, dims), out_shape=(jax.ShapeDtype...]
where the time goes in v3:
time: 76.5 us; the launch traced here: 76.3 us
  Pallas kernels  72.9 us (95%)
  local copies, waits for them, and re-layouts  2.74 us (4%)
    pallas_call x1, Pallas kernels, shards(): pl.pallas_call(functools.partial(kernel, dims), out_shape=(jax.ShapeDtype...  72.9 us
    unnamed x4, local copies, waits for them, and re-layouts  2.74 us

profile of v3, /device:TPU:1, one launch (start us, length us, event | category | flops | bytes accessed | tf_op | source)
XLA Modules:
  0.0 76.3 jit_solution(17492309551229173500)
XLA Ops:
  0.6 72.9 %hybrid.1 = (bf16[128,2048]{1,0:T(8,128)(2,1)}, bf16[128,2048]{1,0:T(8,128)(2,1)}) custom-call(bf16[128,2048]{1,0:T(8,128)(2,1)} %x_far.1, bf16[128,2048]{1,0:T(8,128)(2,1)} %gate_far.1, bf16[128,256]{1,0:T(8,128)(2,1)} %b_far.1, bf16[128,256]{1,0:T(8,128)(2,1)} %c_far.1, f32[32,128]{1,0:T(8,128)} %bitcast.5, f32[1,32]{1,0:T(1,128)} %bitcast.7, ...), custom_call_target="tpu_custom_call" | custom-call | tf_op jit(solution)/shard_map/hybrid/pallas_call | solution.py:845
  73.6 0.0 copy-start
  73.6 1.9 %copy.19 = bf16[128,2048]{1,0:T(8,128)(2,1)} copy(bf16[128,2048]{1,0:T(8,128)(2,1)} %get-tuple-element.4) | data formatting | bytes 1048576
  75.5 0.0 copy-done
  75.5 0.8 %copy.20 = bf16[128,2048]{1,0:T(8,128)(2,1)} copy(bf16[128,2048]{1,0:T(8,128)(2,1)S(1)} %copy-done) | data formatting | bytes 1048576
Async XLA Ops:
  73.6 2.0 %copy-start = (bf16[128,2048]{1,0:T(8,128)(2,1)S(1)}, bf16[128,2048]{1,0:T(8,128)(2,1)}, u32[]{:S(2)}) copy-start(bf16[128,2048]{1,0:T(8,128)(2,1)} %get-tuple-element.5) | copy-start | bytes 1572868

commit v4 on v3

--- a/solution.py
+++ b/solution.py
@@ -432,6 +432,24 @@
         whole_decay[:, at] = per_whole[:8]
 
 
+    HALF = W // 2
+    chunks = W // 128
+
+    def pack(row):
+        parts = [row[:, i * 128 : (i + 1) * 128] for i in range(chunks)]
+        if chunks < 8:
+            parts.append(jnp.ones((8 - chunks, 128), F32))
+        return jnp.concatenate(parts, axis=0)
+
+    for d in [*range(1, Z), 0]:
+        at = pl.ds(pl.multiple_of((z + d) % Z * W, W), W)
+        packed = pack(whole_decay[0:1, at])
+        if d:
+            decay_out[d] = packed
+            start(decay_out.at[d], decay_in.at[z], a2a_send.at[2, d], a2a_recv.at[2, d], z_peer(d))
+        else:
+            decay_in[z] = packed
+
     arrived(tail_x, tail_send.at[0], tail_recv.at[0], before)
     arrived(tail_b, tail_send.at[1], tail_recv.at[1], before)
     arrived(tail_c, tail_send.at[2], tail_recv.at[2], before)
@@ -451,15 +469,6 @@
     pair_arrives(0)
     pair_arrives(1)
 
-    HALF = W // 2
-    chunks = W // 128
-
-    def pack(row):
-        parts = [row[:, i * 128 : (i + 1) * 128] for i in range(chunks)]
-        if chunks < 8:
-            parts.append(jnp.ones((8 - chunks, 128), F32))
-        return jnp.concatenate(parts, axis=0)
-
     def unpack(packed, half):
         return jnp.concatenate(
             [packed[i : i + 1] for i in range(half * chunks // 2, (half + 1) * chunks // 2)], axis=1
@@ -477,14 +486,10 @@
         k = (z + d) % Z
         at = pl.ds(pl.multiple_of(k * W, W), W)
         state = nn(b_turned[k * W // GW], weighted[:, at]).astype(BF16)
-        packed = pack(whole_decay[0:1, at])
         if d:
-            decay_out[d] = packed
             for half in range(2):
                 state_out[half, d] = state[:, half * HALF : (half + 1) * HALF]
-            start(decay_out.at[d], decay_in.at[z], a2a_send.at[2, d], a2a_recv.at[2, d], z_peer(d))
         else:
-            decay_in[z] = packed
             for half in range(2):
                 state_in[half, z] = state[:, half * HALF : (half + 1) * HALF]
 

time: 76.5 us -> 74.8 us (0.978)
  Pallas kernels: 72.9 us -> 71.2 us
    pallas_call x1, Pallas kernels: 72.9 us -> 71.2 us  [shards(): pl.pallas_call(functools.partial(kernel, dims), out_shape=(jax.ShapeDtype...]
where the time goes in v4:
time: 74.8 us; the launch traced here: 74.6 us
  Pallas kernels  71.2 us (95%)
  local copies, waits for them, and re-layouts  2.74 us (4%)
    pallas_call x1, Pallas kernels, shards(): pl.pallas_call(functools.partial(kernel, dims), out_shape=(jax.ShapeDtype...  71.2 us
    unnamed x4, local copies, waits for them, and re-layouts  2.74 us

profile of v4, /device:TPU:1, one launch (start us, length us, event | category | flops | bytes accessed | tf_op | source)
XLA Modules:
  0.0 74.6 jit_solution(11949700373976589506)
XLA Ops:
  0.6 71.2 %hybrid.1 = (bf16[128,2048]{1,0:T(8,128)(2,1)}, bf16[128,2048]{1,0:T(8,128)(2,1)}) custom-call(bf16[128,2048]{1,0:T(8,128)(2,1)} %x_far.1, bf16[128,2048]{1,0:T(8,128)(2,1)} %gate_far.1, bf16[128,256]{1,0:T(8,128)(2,1)} %b_far.1, bf16[128,256]{1,0:T(8,128)(2,1)} %c_far.1, f32[32,128]{1,0:T(8,128)} %bitcast.5, f32[1,32]{1,0:T(1,128)} %bitcast.7, ...), custom_call_target="tpu_custom_call" | custom-call | tf_op jit(solution)/shard_map/hybrid/pallas_call | solution.py:850
  71.9 0.0 copy-start
  71.9 1.9 %copy.19 = bf16[128,2048]{1,0:T(8,128)(2,1)} copy(bf16[128,2048]{1,0:T(8,128)(2,1)} %get-tuple-element.4) | data formatting | bytes 1048576
  73.8 0.0 copy-done
  73.8 0.8 %copy.20 = bf16[128,2048]{1,0:T(8,128)(2,1)} copy(bf16[128,2048]{1,0:T(8,128)(2,1)S(1)} %copy-done) | data formatting | bytes 1048576
Async XLA Ops:
  71.9 2.0 %copy-start = (bf16[128,2048]{1,0:T(8,128)(2,1)S(1)}, bf16[128,2048]{1,0:T(8,128)(2,1)}, u32[]{:S(2)}) copy-start(bf16[128,2048]{1,0:T(8,128)(2,1)} %get-tuple-element.5) | copy-start | bytes 1572868
